TPU v7x, 32 devices: a whole 2x2x4 slice. The times are simulated.
32 devices in a mesh: rep: 4 (over y, core), site: 8 (over z, x).
Axes of the slice: x: 2, y: 2, z: 4, core: 2. Of those that a mesh axis runs over, the one named last changes fastest.
Arguments:
- working: bfloat16 [4, 8, 16, 64, 2304], P('rep', 'site'), may hold values from -4 to 4
- master_slots: float32 [8, 4, 4, 64, 2304], P('site', 'rep'), may hold values from -4 to 4
- accum_slots: float32 [8, 4, 4, 64, 2304], P('site', 'rep'), may hold values from 0.01 to 1
- pool_images: bfloat16 [4, 256, 8, 1024], P(None, None, 'site'), may hold values from -6 to 6
- pool_targets: bfloat16 [4, 8, 16, 64, 256], P(None, 'site'), may hold values from -0.8984375 to 0.8984375
- batch_index: int32 [4, 3], replicated, may hold values from 0 to 3
- owner_map: int32 [4], replicated, may hold values from 0 to 3, each once
Outputs:
- working_next: bfloat16 [8, 16, 64, 2304], P('site')
- master_next: float32 [8, 4, 4, 64, 2304], P('site', 'rep')
- accum_next: float32 [8, 4, 4, 64, 2304], P('site', 'rep')
Inputs may be any that keep to these rules, and one draw needn't show every extreme that they name: `owner_map`: each replica owns exactly one shard.
All inputs are finite; a program needn't handle non-finite values.
Results may differ from a plain program's by a relative error of at most 0.015.
Values may be sent and summed in bfloat16 or wider, within the bound.
No kernel may reach another device: no remote copies, remote signals or barrier semaphores. Data moves between devices by JAX's collectives and lax.ppermute only.
A program may use at most 192 MiB of HBM per device.

v0:
```python
import jax
import jax.numpy as jnp
from jax import lax
from jax.sharding import PartitionSpec as P

CHANNELS = 64
FIELD = 6
MICRO = 3


learning_rate = 0.3
epsilon = 1e-08


def passed_along(shard, axis, by):
    devices = lax.axis_size(axis)
    pairs = [(i, i + by) for i in range(devices) if 0 <= i + by < devices]
    return lax.ppermute(shard, axis, pairs)


def build_patches(window):
    batch_rows = window.shape[0]
    columns = window.shape[2] // CHANNELS
    grid_cells = window.reshape(batch_rows, FIELD, columns, CHANNELS)
    padded = jnp.pad(grid_cells, ((0, 0), (0, 0), (2, 3), (0, 0)))
    stacked = jnp.stack(
        [padded[:, :, offset : offset + columns, :] for offset in range(FIELD)], axis=2
    )
    return stacked.transpose(0, 3, 1, 2, 4).reshape(batch_rows, columns, FIELD * FIELD * CHANNELS)


def halo_rows(images):
    after_one = passed_along(images, "site", -1)
    after_two = passed_along(images, "site", -2)
    after_three = passed_along(images, "site", -3)
    before_one = passed_along(images, "site", 1)
    before_two = passed_along(images, "site", 2)
    return jnp.concatenate(
        [before_two, before_one, images, after_one, after_two, after_three], axis=1
    )


def per_device(
    working, master_slots, accum_slots, pool_images, pool_targets, batch_index, owner_map
):
    replica = lax.axis_index("rep")
    replicas = lax.axis_size("rep")
    chosen = lax.dynamic_index_in_dim(batch_index, replica, 0, keepdims=False)
    weights = working[0, 0]
    factor = weights.shape[2] ** (-0.5)
    gradient = jnp.zeros(weights.shape, jnp.float32)
    for micro_step in range(MICRO):
        images = lax.dynamic_index_in_dim(pool_images, chosen[micro_step], 0, keepdims=False)
        targets = lax.dynamic_index_in_dim(pool_targets, chosen[micro_step], 0, keepdims=False)[0]
        patches = build_patches(halo_rows(images))
        forward = factor * jnp.einsum(
            "bck,cok->cob", patches, weights, preferred_element_type=jnp.float32
        )
        active = jnp.tanh(forward)
        signal = ((active - targets.astype(jnp.float32)) * (1.0 - active * active)).astype(
            jnp.bfloat16
        )
        gradient = gradient + factor * jnp.einsum(
            "cob,bck->cok", signal, patches, preferred_element_type=jnp.float32
        )
    blocks = gradient.reshape(replicas, -1, weights.shape[1], weights.shape[2])
    ordered = jnp.take(blocks, owner_map, axis=0).astype(jnp.bfloat16)
    summed = lax.psum_scatter(ordered, "rep", scatter_dimension=0, tiled=True).astype(jnp.float32)[
        None
    ]
    accum_next = accum_slots + summed * summed
    master_next = master_slots - learning_rate * summed / (jnp.sqrt(accum_next) + epsilon)
    fetched = lax.all_gather(master_next[0].astype(jnp.bfloat16), "rep", axis=0, tiled=True)
    numbers = jnp.arange(replicas, dtype=jnp.int32)
    matches = (owner_map[:, None] == numbers[None, :]).astype(jnp.int32)
    inverse = jnp.sum(numbers[:, None] * matches, axis=0)
    working_next = jnp.take(fetched, inverse, axis=0).reshape(weights.shape)[None]
    return (working_next, master_next, accum_next)


def solution(mesh):
    placed = (
        P("rep", "site", None, None, None),
        P("site", "rep", None, None, None),
        P("site", "rep", None, None, None),
        P(None, None, "site", None),
        P(None, "site", None, None, None),
        P(),
        P(),
    )
    return jax.shard_map(
        per_device,
        mesh=mesh,
        in_specs=placed,
        out_specs=(
            P("site", None, None, None),
            P("site", "rep", None, None, None),
            P("site", "rep", None, None, None),
        ),
        check_vma=False,
    )
```

profile of v0, /device:TPU:3, one launch (start us, length us, event | category | flops | bytes accessed | tf_op | source)
XLA Modules:
  0.0 340.4 jit_solution(14689196669596428532)
XLA Ops:
  16.0 3.2 collective-permute-start
  19.2 3.1 collective-permute-start.1
  22.4 2.9 collective-permute-start.2
  29.7 4.6 %collective-permute-start.5 = (bf16[256,1,1024]{0,2,1:T(8,128)(2,1)S(1)}, bf16[256,1,1024]{0,2,1:T(8,128)(2,1)S(1)}, u32[]{:S(2)}, u32[]{:S(2)}) collective-permute-start(bf16[256,1,1024]{0,2,1:T(8,128)(2,1)S(1)} %bitcast.266), channel_id=1, source_target_pairs={{0,2},{1,3},{2,4},{3,5},{4,6},{5,7},{8,10},{9,11},{10,12},{11,13},... | collective-permute-start | bytes 1572872 | tf_op jit(solution)/shard_map/ppermute | solution.py:18
  34.4 10.5 %collective-permute-done.1 = bf16[256,1,1024]{0,2,1:T(8,128)(2,1)} collective-permute-done((bf16[256,1,1024]{0,2,1:T(8,128)(2,1)S(1)}, bf16[256,1,1024]{0,2,1:T(8,128)(2,1)}, u32[]{:S(2)}, u32[]{:S(2)}) %collective-permute-start.1) | collective-permute-done | bytes 524320 | tf_op jit(solution)/shard_map/ppermute | solution.py:18
  44.9 3.7 %collective-permute-start.6 = (bf16[256,1,1024]{0,2,1:T(8,128)(2,1)S(1)}, bf16[256,1,1024]{0,2,1:T(8,128)(2,1)S(1)}, u32[]{:S(2)}, u32[]{:S(2)}) collective-permute-start(bf16[256,1,1024]{0,2,1:T(8,128)(2,1)S(1)} %bitcast.267), channel_id=1, source_target_pairs={{0,1},{1,2},{2,3},{3,4},{4,5},{5,6},{6,7},{8,9},{9,10},{10,11},{11... | collective-permute-start | bytes 1572872 | tf_op jit(solution)/shard_map/ppermute | solution.py:18
  54.2 18.1 %collective-permute-done.4 = bf16[256,1,1024]{0,2,1:T(8,128)(2,1)} collective-permute-done((bf16[256,1,1024]{0,2,1:T(8,128)(2,1)S(1)}, bf16[256,1,1024]{0,2,1:T(8,128)(2,1)}, u32[]{:S(2)}, u32[]{:S(2)}) %collective-permute-start.4) | collective-permute-done | bytes 524320 | tf_op jit(solution)/shard_map/ppermute | solution.py:18
  80.2 7.0 %collective-permute-start.10 = (bf16[256,1,1024]{0,2,1:T(8,128)(2,1)S(1)}, bf16[256,1,1024]{0,2,1:T(8,128)(2,1)S(1)}, u32[]{:S(2)}, u32[]{:S(2)}) collective-permute-start(bf16[256,1,1024]{0,2,1:T(8,128)(2,1)S(1)} %bitcast.259), channel_id=1, source_target_pairs={{0,2},{1,3},{2,4},{3,5},{4,6},{5,7},{8,10},{9,11},{10,12},{11,13},... | collective-permute-start | bytes 1572872 | tf_op jit(solution)/shard_map/ppermute | solution.py:18
  87.2 6.8 %copy.96 = bf16[256,16,6,6,64]{0,4,3,2,1:T(8,128)(2,1)} copy(bf16[256,16,6,6,64]{0,4,1,2,3:T(8,128)(2,1)S(1)} %bitcast.254) | data formatting | bytes 37748736 | tf_op jit(solution)/shard_map/transpose | solution.py:29
  94.0 3.1 collective-permute-start.11
  97.1 2.2 collective-permute-start.12
  100.8 17.3 %collective-permute-done.9 = bf16[256,1,1024]{0,2,1:T(8,128)(2,1)S(1)} collective-permute-done((bf16[256,1,1024]{0,2,1:T(8,128)(2,1)S(1)}, bf16[256,1,1024]{0,2,1:T(8,128)(2,1)S(1)}, u32[]{:S(2)}, u32[]{:S(2)}) %collective-permute-start.9) | collective-permute-done | bytes 524320 | tf_op jit(solution)/shard_map/ppermute | solution.py:18
  122.1 6.7 %copy.107 = bf16[256,16,6,6,64]{0,4,3,2,1:T(8,128)(2,1)} copy(bf16[256,16,6,6,64]{0,4,1,2,3:T(8,128)(2,1)S(1)} %bitcast.255) | data formatting | bytes 37748736 | tf_op jit(solution)/shard_map/transpose | solution.py:29
  128.8 24.2 %fusion.77 = f32[16,64,2304]{2,1,0:T(8,128)} fusion(bf16[256,16,2304]{0,2,1:T(8,128)(2,1)} %bitcast.251, bf16[1,1,16,64,2304]{4,3,2,1,0:T(8,128)(2,1)} %param.7, bf16[4,1,16,64,256]{4,3,2,1,0:T(8,128)(2,1)} %param.11, s32[]{:T(128)S(6)} %select_n.56), kind=kOutput, calls=%fused_computation.81 | convolution fusion | flops 2417754112 | bytes 52428804 | tf_op jit(solution)/shard_map/cob,bck->cok/dot_general | solution.py:63
  153.0 24.2 %fusion.82 = f32[16,64,2304]{2,1,0:T(8,128)} fusion(bf16[256,16,2304]{0,2,1:T(8,128)(2,1)} %bitcast.252, bf16[1,1,16,64,2304]{4,3,2,1,0:T(8,128)(2,1)} %param.7, bf16[4,1,16,64,256]{4,3,2,1,0:T(8,128)(2,1)} %param.11, s32[]{:T(128)S(6)} %select_n.57), kind=kOutput, calls=%fused_computation.82 | convolution fusion | flops 2417754112 | bytes 52428804 | tf_op jit(solution)/shard_map/cob,bck->cok/dot_general | solution.py:63
  182.0 6.7 %copy.118 = bf16[256,16,6,6,64]{0,4,3,2,1:T(8,128)(2,1)} copy(bf16[256,16,6,6,64]{0,4,1,2,3:T(8,128)(2,1)S(1)} %bitcast.256) | data formatting | bytes 37748736 | tf_op jit(solution)/shard_map/transpose | solution.py:29
  188.8 25.7 %add_multiply_fusion = bf16[16,64,2304]{2,1,0:T(8,128)(2,1)} fusion(f32[16,64,2304]{2,1,0:T(8,128)} %fusion.77, f32[16,64,2304]{2,1,0:T(8,128)} %fusion.82, bf16[256,16,2304]{0,2,1:T(8,128)(2,1)} %bitcast.250, bf16[1,1,16,64,2304]{4,3,2,1,0:T(8,128)(2,1)} %param.7, bf16[4,1,16,64,256]{4,3,2,1,0:T(8,128)(2,1)} %param.11, s32[]{:T(128)S(6)} %select_n.58), kind=kOutput, calls=%fused_computation.2 | convolution fusion | flops 2427191296 | bytes 66584580 | tf_op jit(solution)/shard_map/cob,bck->cok/dot_general | solution.py:63
  214.5 5.3 %gather_fusion = bf16[4,4,64,2304]{3,2,1,0:T(8,128)(2,1)} fusion(bf16[4,4,64,2304]{3,2,1,0:T(8,128)(2,1)} %bitcast.253, s32[1024]{0:T(1024)S(1)} %pad_clamp_fusion.1), kind=kCustom, calls=%fused_computation | custom fusion | bytes 9437200 | tf_op jit(solution)/shard_map/jit(_take)/gather | solution.py:67
  219.8 5.6 %select_convert_fusion = bf16[4,4,64,2304]{3,2,1,0:T(8,128)(2,1)} fusion(bf16[4,4,64,2304]{3,2,1,0:T(8,128)(2,1)} %gather_fusion, pred[4]{0:T(512)(128)(4,1)S(1)} %compare_and_fusion), kind=kLoop, calls=%fused_computation.3 | loop fusion | flops 2359296 | bytes 9437188 | tf_op jit(solution)/shard_map/convert_element_type | solution.py:67
  225.5 53.7 %reduce-scatter.2.cloned.1.call-done = bf16[1,4,64,2304]{3,2,1,0:T(8,128)(2,1)} async-done(((bf16[4,4,64,2304]{3,2,1,0:T(8,128)(2,1)}), bf16[1,4,64,2304]{3,2,1,0:T(8,128)(2,1)}) %reduce-scatter.2.cloned.1.call-update) | async-done | bytes 1179664 | tf_op jit(solution)/shard_map/reduce_scatter | solution.py:68
  279.2 5.8 %fusion.110 = (bf16[1,1,4,64,2304]{4,3,2,1,0:T(8,128)(2,1)}, f32[1,1,4,64,2304]{4,3,2,1,0:T(8,128)}, f32[1,1,4,64,2304]{4,3,2,1,0:T(8,128)}) fusion(f32[1,1,4,64,2304]{4,3,2,1,0:T(8,128)S(1)} %copy-done.2, bf16[1,4,64,2304]{3,2,1,0:T(8,128)(2,1)} %reduce-scatter.2.cloned.1.call-done, f32[1,1,4,64,2304]{4,3,2,1,0:T(8,128)} %param.9), kind=kLoop, calls=%fused_computation.154 | loop fusion | flops 4718592 | bytes 11796480 | tf_op jit(solution)/shard_map/convert_element_type | solution.py:73
  285.2 37.9 %all-gather.3.cloned.1.call-done = bf16[4,1,4,64,2304]{4,3,2,1,0:T(8,128)(2,1)} async-done(((bf16[1,1,4,64,2304]{4,3,2,1,0:T(8,128)(2,1)}), bf16[4,1,4,64,2304]{4,3,2,1,0:T(8,128)(2,1)}) %all-gather.3.cloned.1.call-update) | async-done | bytes 4718608 | tf_op jit(solution)/shard_map/all_gather | solution.py:73
  323.1 5.4 %gather_fusion.1 = bf16[4,4,64,2304]{3,2,1,0:T(8,128)(2,1)} fusion(bf16[4,4,64,2304]{3,2,1,0:T(8,128)(2,1)} %bitcast.258, s32[1024]{0:T(1024)S(1)} %pad_clamp_fusion), kind=kCustom, calls=%fused_computation.1 | custom fusion | bytes 9437200 | tf_op jit(solution)/shard_map/jit(_take)/gather | solution.py:77
  328.5 5.0 %bitcast_select_fusion = bf16[1,16,64,2304]{3,2,1,0:T(8,128)(2,1)} fusion(pred[16]{0:T(512)(128)(4,1)S(1)} %broadcast_in_dim.31, bf16[1,16,64,2304]{3,2,1,0:T(8,128)(2,1)} %bitcast.257), kind=kLoop, calls=%fused_computation.4 | loop fusion | flops 2359296 | bytes 9437200 | tf_op jit(solution)/shard_map/jit(_take)/select_n | solution.py:77
  (97 shorter events, 31.0 us)
Async XLA Ops:
  7.2 0.7 copy-start
  7.2 272.0 %reduce-scatter.2.cloned.1.call-start = ((), (), s32[]{:S(2)}) async-start(), calls=%async_computation.1 | async-start | bytes 5898240 | tf_op jit(solution)/shard_map/reduce_scatter | solution.py:68
  16.0 13.7 %collective-permute-start = (bf16[256,1,1024]{0,2,1:T(8,128)(2,1)S(1)}, bf16[256,1,1024]{0,2,1:T(8,128)(2,1)S(1)}, u32[]{:S(2)}, u32[]{:S(2)}) collective-permute-start(bf16[256,1,1024]{0,2,1:T(8,128)(2,1)S(1)} %bitcast.273), channel_id=1, source_target_pairs={{0,2},{1,3},{2,4},{3,5},{4,6},{5,7},{8,10},{9,11},{10,12},{11,13},... | collective-permute-start | bytes 1572872 | tf_op jit(solution)/shard_map/ppermute | solution.py:18
  19.2 25.7 %collective-permute-start.1 = (bf16[256,1,1024]{0,2,1:T(8,128)(2,1)S(1)}, bf16[256,1,1024]{0,2,1:T(8,128)(2,1)}, u32[]{:S(2)}, u32[]{:S(2)}) collective-permute-start(bf16[256,1,1024]{0,2,1:T(8,128)(2,1)S(1)} %bitcast.274), channel_id=1, source_target_pairs={{0,1},{1,2},{2,3},{3,4},{4,5},{5,6},{6,7},{8,9},{9,10},{10,11},{11... | collective-permute-start | bytes 1572872 | tf_op jit(solution)/shard_map/ppermute | solution.py:18
  22.4 27.4 %collective-permute-start.2 = (bf16[256,1,1024]{0,2,1:T(8,128)(2,1)S(1)}, bf16[256,1,1024]{0,2,1:T(8,128)(2,1)S(1)}, u32[]{:S(2)}, u32[]{:S(2)}) collective-permute-start(bf16[256,1,1024]{0,2,1:T(8,128)(2,1)S(1)} %bitcast.275), channel_id=1, source_target_pairs={{1,0},{2,1},{3,2},{4,3},{5,4},{6,5},{7,6},{9,8},{10,9},{11,10},{12... | collective-permute-start | bytes 1572872 | tf_op jit(solution)/shard_map/ppermute | solution.py:18
  25.3 26.5 %collective-permute-start.3 = (bf16[256,1,1024]{0,2,1:T(8,128)(2,1)S(1)}, bf16[256,1,1024]{0,2,1:T(8,128)(2,1)}, u32[]{:S(2)}, u32[]{:S(2)}) collective-permute-start(bf16[256,1,1024]{0,2,1:T(8,128)(2,1)S(1)} %bitcast.276), channel_id=1, source_target_pairs={{2,0},{3,1},{4,2},{5,3},{6,4},{7,5},{10,8},{11,9},{12,10},{13,11},... | collective-permute-start | bytes 1572872 | tf_op jit(solution)/shard_map/ppermute | solution.py:18
  26.6 45.6 %collective-permute-start.4 = (bf16[256,1,1024]{0,2,1:T(8,128)(2,1)S(1)}, bf16[256,1,1024]{0,2,1:T(8,128)(2,1)}, u32[]{:S(2)}, u32[]{:S(2)}) collective-permute-start(bf16[256,1,1024]{0,2,1:T(8,128)(2,1)S(1)} %bitcast.277), channel_id=1, source_target_pairs={{3,0},{4,1},{5,2},{6,3},{7,4},{11,8},{12,9},{13,10},{14,11},{15,12... | collective-permute-start | bytes 1572872 | tf_op jit(solution)/shard_map/ppermute | solution.py:18
  29.7 50.5 %collective-permute-start.5 = (bf16[256,1,1024]{0,2,1:T(8,128)(2,1)S(1)}, bf16[256,1,1024]{0,2,1:T(8,128)(2,1)S(1)}, u32[]{:S(2)}, u32[]{:S(2)}) collective-permute-start(bf16[256,1,1024]{0,2,1:T(8,128)(2,1)S(1)} %bitcast.266), channel_id=1, source_target_pairs={{0,2},{1,3},{2,4},{3,5},{4,6},{5,7},{8,10},{9,11},{10,12},{11,13},... | collective-permute-start | bytes 1572872 | tf_op jit(solution)/shard_map/ppermute | solution.py:18
  44.9 49.1 %collective-permute-start.6 = (bf16[256,1,1024]{0,2,1:T(8,128)(2,1)S(1)}, bf16[256,1,1024]{0,2,1:T(8,128)(2,1)S(1)}, u32[]{:S(2)}, u32[]{:S(2)}) collective-permute-start(bf16[256,1,1024]{0,2,1:T(8,128)(2,1)S(1)} %bitcast.267), channel_id=1, source_target_pairs={{0,1},{1,2},{2,3},{3,4},{4,5},{5,6},{6,7},{8,9},{9,10},{10,11},{11... | collective-permute-start | bytes 1572872 | tf_op jit(solution)/shard_map/ppermute | solution.py:18
  49.8 47.4 %collective-permute-start.7 = (bf16[256,1,1024]{0,2,1:T(8,128)(2,1)S(1)}, bf16[256,1,1024]{0,2,1:T(8,128)(2,1)S(1)}, u32[]{:S(2)}, u32[]{:S(2)}) collective-permute-start(bf16[256,1,1024]{0,2,1:T(8,128)(2,1)S(1)} %bitcast.268), channel_id=1, source_target_pairs={{1,0},{2,1},{3,2},{4,3},{5,4},{6,5},{7,6},{9,8},{10,9},{11,10},{12... | collective-permute-start | bytes 1572872 | tf_op jit(solution)/shard_map/ppermute | solution.py:18
  51.8 47.7 %collective-permute-start.8 = (bf16[256,1,1024]{0,2,1:T(8,128)(2,1)S(1)}, bf16[256,1,1024]{0,2,1:T(8,128)(2,1)S(1)}, u32[]{:S(2)}, u32[]{:S(2)}) collective-permute-start(bf16[256,1,1024]{0,2,1:T(8,128)(2,1)S(1)} %bitcast.269), channel_id=1, source_target_pairs={{2,0},{3,1},{4,2},{5,3},{6,4},{7,5},{10,8},{11,9},{12,10},{13,11},... | collective-permute-start | bytes 1572872 | tf_op jit(solution)/shard_map/ppermute | solution.py:18
  72.2 45.9 %collective-permute-start.9 = (bf16[256,1,1024]{0,2,1:T(8,128)(2,1)S(1)}, bf16[256,1,1024]{0,2,1:T(8,128)(2,1)S(1)}, u32[]{:S(2)}, u32[]{:S(2)}) collective-permute-start(bf16[256,1,1024]{0,2,1:T(8,128)(2,1)S(1)} %bitcast.270), channel_id=1, source_target_pairs={{3,0},{4,1},{5,2},{6,3},{7,4},{11,8},{12,9},{13,10},{14,11},{15,12... | collective-permute-start | bytes 1572872 | tf_op jit(solution)/shard_map/ppermute | solution.py:18
  80.2 97.0 %collective-permute-start.10 = (bf16[256,1,1024]{0,2,1:T(8,128)(2,1)S(1)}, bf16[256,1,1024]{0,2,1:T(8,128)(2,1)S(1)}, u32[]{:S(2)}, u32[]{:S(2)}) collective-permute-start(bf16[256,1,1024]{0,2,1:T(8,128)(2,1)S(1)} %bitcast.259), channel_id=1, source_target_pairs={{0,2},{1,3},{2,4},{3,5},{4,6},{5,7},{8,10},{9,11},{10,12},{11,13},... | collective-permute-start | bytes 1572872 | tf_op jit(solution)/shard_map/ppermute | solution.py:18
  94.0 83.3 %collective-permute-start.11 = (bf16[256,1,1024]{0,2,1:T(8,128)(2,1)S(1)}, bf16[256,1,1024]{0,2,1:T(8,128)(2,1)S(1)}, u32[]{:S(2)}, u32[]{:S(2)}) collective-permute-start(bf16[256,1,1024]{0,2,1:T(8,128)(2,1)S(1)} %bitcast.260), channel_id=1, source_target_pairs={{0,1},{1,2},{2,3},{3,4},{4,5},{5,6},{6,7},{8,9},{9,10},{10,11},{11... | collective-permute-start | bytes 1572872 | tf_op jit(solution)/shard_map/ppermute | solution.py:18
  97.1 80.2 %collective-permute-start.12 = (bf16[256,1,1024]{0,2,1:T(8,128)(2,1)S(1)}, bf16[256,1,1024]{0,2,1:T(8,128)(2,1)S(1)}, u32[]{:S(2)}, u32[]{:S(2)}) collective-permute-start(bf16[256,1,1024]{0,2,1:T(8,128)(2,1)S(1)} %bitcast.261), channel_id=1, source_target_pairs={{1,0},{2,1},{3,2},{4,3},{5,4},{6,5},{7,6},{9,8},{10,9},{11,10},{12... | collective-permute-start | bytes 1572872 | tf_op jit(solution)/shard_map/ppermute | solution.py:18
  99.5 78.0 %collective-permute-start.13 = (bf16[256,1,1024]{0,2,1:T(8,128)(2,1)S(1)}, bf16[256,1,1024]{0,2,1:T(8,128)(2,1)S(1)}, u32[]{:S(2)}, u32[]{:S(2)}) collective-permute-start(bf16[256,1,1024]{0,2,1:T(8,128)(2,1)S(1)} %bitcast.262), channel_id=1, source_target_pairs={{2,0},{3,1},{4,2},{5,3},{6,4},{7,5},{10,8},{11,9},{12,10},{13,11},... | collective-permute-start | bytes 1572872 | tf_op jit(solution)/shard_map/ppermute | solution.py:18
  118.1 59.3 %collective-permute-start.14 = (bf16[256,1,1024]{0,2,1:T(8,128)(2,1)S(1)}, bf16[256,1,1024]{0,2,1:T(8,128)(2,1)}, u32[]{:S(2)}, u32[]{:S(2)}) collective-permute-start(bf16[256,1,1024]{0,2,1:T(8,128)(2,1)S(1)} %bitcast.263), channel_id=1, source_target_pairs={{3,0},{4,1},{5,2},{6,3},{7,4},{11,8},{12,9},{13,10},{14,11},{15,12... | collective-permute-start | bytes 1572872 | tf_op jit(solution)/shard_map/ppermute | solution.py:18
  225.4 53.8 %copy-start.2 = (f32[1,1,4,64,2304]{4,3,2,1,0:T(8,128)S(1)}, f32[1,1,4,64,2304]{4,3,2,1,0:T(8,128)}, u32[]{:S(2)}) copy-start(f32[1,1,4,64,2304]{4,3,2,1,0:T(8,128)} %param.8) | copy-start | bytes 7077892
  225.4 59.5 %copy-start.3 = (s32[4]{0:T(128)S(1)}, s32[4]{0:T(128)}, u32[]{:S(2)}) copy-start(s32[4]{0:T(128)} %param.13) | copy-start | bytes 52
  225.4 97.7 %all-gather.3.cloned.1.call-start = ((), (), s32[]{:S(2)}) async-start(), calls=%async_computation.2 | async-start | bytes 5898240 | tf_op jit(solution)/shard_map/all_gather | solution.py:73
  328.5 5.1 %copy-start.1 = (s32[4,3]{1,0:T(4,128)S(1)}, s32[4,3]{1,0:T(4,128)}, u32[]{:S(2)}) copy-start(s32[4,3]{1,0:T(4,128)} %param.12) | copy-start | bytes 148
Sparse Core Ops, SparseCore 0:
  225.6 53.5 reduce-scatter.1
  285.1 38.0 all-gather.2
where the time goes:
time: 343 us; the launch traced here: 340 us
  waiting for transfers between devices  138 us (40%)
  matrix products  74.1 us (22%)
  local copies, waits for them, and re-layouts  50.5 us (15%)
  starting transfers between devices  39.8 us (12%)
  between operations  20.5 us (6%)
  other arithmetic  17.9 us (5%)
    dot_general x3, matrix products, per_device(): jnp.einsum('cob,bck->cok', signal, patches, preferred_element_type=jnp.fl...  74.1 us
    reduce_scatter x1, waiting for transfers between devices, per_device(): lax.psum_scatter(ordered, 'rep', scatter_dimension=0, tiled=True)  53.7 us
    ppermute x15, waiting for transfers between devices, passed_along(): return lax.ppermute(shard, axis, pairs)  46 us
    ppermute x15, starting transfers between devices, passed_along(): return lax.ppermute(shard, axis, pairs)  39.7 us
    all_gather x1, waiting for transfers between devices, per_device(): lax.all_gather(master_next[0].astype(jnp.bfloat16), 'rep', axis=0, tiled=...  37.9 us
    transpose x3, local copies, waits for them, and re-layouts, build_patches(): stacked.transpose(0, 3, 1, 2, 4)  20.2 us
    unnamed x56, local copies, waits for them, and re-layouts  13.9 us
  transfers between devices with their start and end apart: 17, of which 5 were waited for; matrix products, arithmetic and copies ran while one was open for 22% of the time, Pallas kernels for 0%

commit v1 on v0

v1 whole, which is shorter than its diff:
```python
import functools

import jax
import jax.numpy as jnp
from jax import lax
from jax.experimental import pallas as pl
from jax.experimental.pallas import tpu as pltpu
from jax.sharding import PartitionSpec as P

FIELD = 6
BEFORE = 2
MICRO = 3

learning_rate = 0.3
epsilon = 1e-08

ANY = pl.BlockSpec(memory_space=pl.ANY)
SMEM = pl.BlockSpec(memory_space=pltpu.SMEM)
VMEM_LIMIT = 56 * 1024 * 1024


def moved(x, axis, target):
    n = lax.axis_size(axis)
    pairs = [(i, target(i)) for i in range(n)]
    return lax.ppermute(x, axis, [(i, t) for i, t in pairs if t is not None and 0 <= t < n])


def sizes_of(geo):
    maps, cols, block, channels = geo
    window = -(-(block + FIELD - 1) * channels // 128) * 128
    return maps, cols, block, channels, window


def window_cases(geo):
    maps, cols, block, channels, window = sizes_of(geo)
    cases = []
    for shard in range(cols // block):
        first = shard * block * channels - BEFORE * channels
        lo, hi = max(first, 0), min(first + window, cols * channels)
        cases.append((lo, hi - lo, lo - first))
    return cases


def load_rows(info, geo, drs, near, own, dst, sem):
    window = sizes_of(geo)[-1]
    half = own.shape[0] // 2
    shard, odd, core = info[0], info[1], info[2]
    here, there = core * half, (1 - core) * half

    def both(case, at, pair):
        lo, width, to = case
        dst_lanes = pl.ds(at + to, width)
        for start, ref in zip((here, there), pair):
            pltpu.make_async_copy(
                ref.at[:, :, pl.ds(lo, width)], dst.at[pl.ds(start, half), :, dst_lanes], sem
            ).start()

    for number, case in enumerate(window_cases(geo)):

        @pl.when(shard == number)
        def _(case=case):
            lo, width, to = case
            for place, dr in enumerate(drs):
                at = place * window
                if dr == BEFORE:
                    pltpu.make_async_copy(
                        own.at[:, :, pl.ds(lo, width)], dst.at[:, :, pl.ds(at + to, width)], sem
                    ).start()
                    continue
                even_pair, odd_pair = near[dr]
                if even_pair is odd_pair:
                    both(case, at, even_pair)
                else:

                    @pl.when(odd == 0)
                    def _():
                        both(case, at, even_pair)

                    @pl.when(odd == 1)
                    def _():
                        both(case, at, odd_pair)


def wait_rows(info, geo, drs, dst, sem):
    for number, (_, width, _) in enumerate(window_cases(geo)):

        @pl.when(info[0] == number)
        def _(width=width):
            taken = dst.at[:, :, pl.ds(0, len(drs) * width)]
            pltpu.make_async_copy(taken, taken, sem).wait()


def clear_edges(geo, drs, dst):
    window = sizes_of(geo)[-1]
    zero_lanes = set()
    for lo, width, to in window_cases(geo):
        zero_lanes |= set(range(0, to, 128)) | set(range(to + width, window, 128))
    for place in range(len(drs)):
        for lane in sorted(zero_lanes):
            dst[:, :, place * window + lane : place * window + lane + 128] = jnp.zeros(
                dst.shape[:2] + (128,), dst.dtype
            )


def band(geo, drs, weights, wide):
    maps, cols, block, channels, window = sizes_of(geo)
    span = FIELD * channels
    for place in range(len(drs)):
        for p in range(block):
            w = weights[p, :, place * span : (place + 1) * span]
            parts = []
            if p:
                parts.append(jnp.zeros((maps, p * channels), w.dtype))
            parts.append(w)
            parts.append(jnp.zeros((maps, window - span - p * channels), w.dtype))
            wide[p * maps : (p + 1) * maps, place * window : (place + 1) * window] = (
                jnp.concatenate(parts, axis=1)
            )


NT = (((1,), (1,)), ((), ()))


def forward_kernel(geo, drs, last, n_near, factor, *refs):
    info, choice = refs[0], refs[1]
    own = refs[2]
    flat = refs[3 : 3 + n_near]
    w_refs = refs[3 + n_near : 7 + n_near]
    rest = refs[7 + n_near :]
    if last:
        before, targets, out, xs, wb, wide, tb, pb, sem, wsem, tsem = rest
    else:
        out, xs, wb, wide, sem, wsem = rest
    near = unflatten(drs, flat)
    maps, cols, block, channels, window = sizes_of(geo)
    span = FIELD * channels
    lanes = pl.ds(drs[0] * span, len(drs) * span)
    copies = []
    for k in range(4):
        if k == 0:
            src = w_refs[0].at[pl.ds(info[0] * block, block), :, lanes]
        else:
            src = w_refs[k].at[:, :, lanes]
        copies.append(pltpu.make_async_copy(src, wb.at[k], wsem.at[k]))
        copies[-1].start()
    if last:
        t_copy = pltpu.make_async_copy(
            targets.at[:, pl.ds(info[0] * block * maps, block * maps), :], tb, tsem.at[0]
        )
        p_copy = pltpu.make_async_copy(before, pb, tsem.at[1])
        t_copy.start()
        p_copy.start()
    clear_edges(geo, drs, xs)
    load_rows(info, geo, drs, near, own, xs, sem)
    for c in copies:
        c.wait()
    if last:
        t_copy.wait()
        p_copy.wait()
    wait_rows(info, geo, drs, xs, sem)

    def per_replica(k, carry):
        band(geo, drs, wb.at[k], wide)

        def per_step(m, carry):
            q = choice[k * MICRO + m]
            pre = lax.dot_general(wide[...], xs[q], NT, preferred_element_type=jnp.float32)
            at = k * MICRO + m
            if last:
                act = jnp.tanh(factor * (pre + pb[at]))
                sig = (act - tb[q].astype(jnp.float32)) * (1.0 - act * act)
                out[at] = sig.astype(out.dtype)
            else:
                out[at] = pre
            return carry

        return lax.fori_loop(0, MICRO, per_step, carry)

    lax.fori_loop(0, 4, per_replica, 0)


def backward_kernel(geo, drs, n_near, n_alias, factor, *refs):
    info, choice, own = refs[0], refs[1], refs[2]
    flat = refs[3 : 3 + n_near]
    sig, master, accum = refs[3 + n_near : 6 + n_near]
    rest = refs[6 + n_near + n_alias :]
    shard_out, master_out, accum_out, xs, total, sem = rest
    near = unflatten(drs, flat)
    maps, cols, block, channels, window = sizes_of(geo)
    span = FIELD * channels
    clear_edges(geo, drs, xs)
    load_rows(info, geo, drs, near, own, xs, sem)
    wait_rows(info, geo, drs, xs, sem)
    total[...] = jnp.zeros_like(total)

    def per_replica(k, carry):
        acc = None
        for m in range(MICRO):
            q = choice[k * MICRO + m]
            part = jnp.dot(sig[k * MICRO + m], xs[q], preferred_element_type=jnp.float32)
            acc = part if acc is None else acc + part
        total[...] += (factor * acc).astype(jnp.bfloat16).astype(jnp.float32)
        return carry

    lax.fori_loop(0, 4, per_replica, 0)
    for place in range(len(drs)):
        for p in range(block):
            at = place * window + p * channels
            slot = total[p * maps : (p + 1) * maps, at : at + span]
            here = slice(place * span, (place + 1) * span)
            grown = accum[p, :, here] + slot * slot
            new = master[p, :, here] - learning_rate * slot / (jnp.sqrt(grown) + epsilon)
            accum_out[p, :, here] = grown
            master_out[p, :, here] = new
            shard_out[p, :, here] = new.astype(jnp.bfloat16)


def near_for(drs, rows):
    flat = []
    for dr in drs:
        if dr != BEFORE:
            even_pair, odd_pair = rows[dr]
            flat += list(even_pair)
            if odd_pair is not even_pair:
                flat += list(odd_pair)
    return flat


TWO_SOURCES = (1, 3, 5)


def unflatten(drs, flat):
    near, at = {}, 0
    for dr in drs:
        if dr == BEFORE:
            continue
        even_pair = (flat[at], flat[at + 1])
        at += 2
        odd_pair = even_pair
        if dr in TWO_SOURCES:
            odd_pair = (flat[at], flat[at + 1])
            at += 2
        near[dr] = (even_pair, odd_pair)
    return near


def forward(geo, drs, factor, info, choice, own, rows, w_blocks, before=None, targets=None):
    maps, cols, block, channels, window = sizes_of(geo)
    pool, batch, _ = own.shape
    flat = near_for(drs, rows)
    last = before is not None
    tall = block * maps
    scratch = [
        pltpu.VMEM((pool, batch, len(drs) * window), own.dtype),
        pltpu.VMEM((4, block, maps, len(drs) * FIELD * channels), own.dtype),
        pltpu.VMEM((tall, len(drs) * window), own.dtype),
    ]
    inputs = [info, choice, own, *flat, *w_blocks]
    if last:
        scratch += [
            pltpu.VMEM((pool, tall, batch), targets.dtype),
            pltpu.VMEM((4 * MICRO, tall, batch), jnp.float32),
        ]
        inputs += [before, targets]
    scratch += [pltpu.SemaphoreType.DMA, pltpu.SemaphoreType.DMA((4,))]
    if last:
        scratch += [pltpu.SemaphoreType.DMA((2,))]
    return pl.pallas_call(
        functools.partial(forward_kernel, geo, drs, last, len(flat), factor),
        out_shape=jax.ShapeDtypeStruct(
            (4 * MICRO, tall, batch), own.dtype if last else jnp.float32
        ),
        in_specs=[SMEM, SMEM] + [ANY] * (len(inputs) - 2),
        out_specs=pl.BlockSpec(memory_space=pltpu.VMEM),
        scratch_shapes=scratch,
        compiler_params=pltpu.CompilerParams(vmem_limit_bytes=VMEM_LIMIT),
        cost_estimate=pl.CostEstimate(
            flops=2 * 12 * tall * batch * len(drs) * window, transcendentals=0, bytes_accessed=8 << 20
        ),
        name="forward",
    )(*inputs)


def backward(geo, drs, factor, info, choice, own, rows, sig, master, accum, outs):
    maps, cols, block, channels, window = sizes_of(geo)
    pool, batch, _ = own.shape
    span = FIELD * channels
    flat = near_for(drs, rows)
    tall = block * maps
    j = drs[0] // len(drs)
    lanes = pl.BlockSpec((block, maps, len(drs) * span), lambda i: (0, 0, j))
    n_in = 3 + len(flat) + 3
    n_alias = 0 if outs is None else 2
    whole = jax.ShapeDtypeStruct(master.shape, jnp.float32)
    return pl.pallas_call(
        functools.partial(backward_kernel, geo, drs, len(flat), n_alias, factor),
        grid=(1,),
        out_shape=(
            jax.ShapeDtypeStruct((block, maps, len(drs) * span), jnp.bfloat16),
            whole,
            whole,
        ),
        in_specs=[SMEM, SMEM]
        + [ANY] * (1 + len(flat))
        + [pl.BlockSpec(sig.shape, lambda i: (0, 0, 0)), lanes, lanes]
        + [ANY] * n_alias,
        out_specs=(
            pl.BlockSpec((block, maps, len(drs) * span), lambda i: (0, 0, 0)),
            lanes,
            lanes,
        ),
        input_output_aliases={} if outs is None else {n_in: 1, n_in + 1: 2},
        scratch_shapes=[
            pltpu.VMEM((pool, batch, len(drs) * window), own.dtype),
            pltpu.VMEM((tall, len(drs) * window), jnp.float32),
            pltpu.SemaphoreType.DMA,
        ],
        compiler_params=pltpu.CompilerParams(vmem_limit_bytes=VMEM_LIMIT),
        cost_estimate=pl.CostEstimate(
            flops=2 * 12 * tall * batch * len(drs) * window, transcendentals=0, bytes_accessed=8 << 20
        ),
        name="backward",
    )(info, choice, own, *flat, sig, master, accum, *(outs or ()))


def place_kernel(first_lane, block, shards, *refs):
    a = refs[1:5]
    out, sem = refs[-2:]
    copies = [
        pltpu.make_async_copy(
            a[k],
            out.at[pl.ds(refs[0][k] * block, block), :, pl.ds(first_lane, a[k].shape[2])],
            sem.at[k],
        )
        for k in range(4)
    ]
    for c in copies:
        c.start()
    for c in copies:
        c.wait()


def place(shards, pieces, first_lane, shape, out):
    block = pieces[0].shape[0]
    extra = [] if out is None else [out]
    return pl.pallas_call(
        functools.partial(place_kernel, first_lane, block, 4),
        out_shape=jax.ShapeDtypeStruct(shape, jnp.bfloat16),
        in_specs=[SMEM] + [ANY] * (4 + len(extra)),
        out_specs=ANY,
        input_output_aliases={5: 0} if extra else {},
        scratch_shapes=[pltpu.SemaphoreType.DMA((4,))],
        name="place",
    )(shards, *pieces, *extra)


def per_device(
    working, master_slots, accum_slots, pool_images, pool_targets, batch_index, owner_map
):
    rep = lax.axis_index("rep")
    site = lax.axis_index("site")
    replicas = lax.axis_size("rep")
    weights = working[0, 0]
    cols, maps, depth = weights.shape
    factor = depth ** (-0.5)
    block = cols // replicas
    pool, batch, _, lanes = pool_images.shape
    geo = (maps, cols, block, lanes // cols)
    own = pool_images.reshape(pool, batch, lanes)
    targets = pool_targets.reshape(pool, cols * maps, batch)
    peers = [rep ^ k for k in range(replicas)]
    shards = jnp.stack([owner_map[p] for p in peers]).astype(jnp.int32)
    choice = jnp.concatenate([batch_index[p] for p in peers]).astype(jnp.int32)
    core = rep % 2
    info = jnp.stack([shards[0], site % 2, core]).astype(jnp.int32)

    half = lax.dynamic_slice_in_dim(own, core * (pool // 2), pool // 2, 0)
    beside = moved(half, "site", lambda i: i ^ 1)
    from_before = moved(half, "site", lambda i: i + 2)
    from_after = moved(half, "site", lambda i: i - 2)
    w_blocks = [weights]
    for k in range(1, replicas):
        piece = lax.dynamic_slice_in_dim(weights, shards[k] * block, block, 0)
        w_blocks.append(moved(piece, "rep", lambda i, k=k: i ^ k))
    further_before = moved(beside, "site", lambda i: i + 2 if i % 2 == 0 else None)
    further_after = moved(beside, "site", lambda i: i - 2)
    last_after = moved(from_after, "site", lambda i: i - 1 if i % 2 == 0 else None)

    def pair(x):
        return (x, moved(x, "rep", lambda i: i ^ 1))

    beside, from_before, from_after, further_before, further_after, last_after = [
        pair(x)
        for x in (beside, from_before, from_after, further_before, further_after, last_after)
    ]
    rows = {
        0: (from_before, from_before),
        1: (further_before, beside),
        3: (beside, further_after),
        4: (from_after, from_after),
        5: (further_after, last_after),
    }
    partial = forward(geo, (0, 1, 2, 3, 4), factor, info, choice, own, rows, w_blocks)
    signal = forward(
        geo, (5,), factor, info, choice, own, rows, w_blocks, partial, targets
    )
    outs = None
    working_next = None
    for drs in ((0, 1), (2, 3), (4, 5)):
        fresh, *outs = backward(
            geo, drs, factor, info, choice, own, rows, signal, master_slots[0, 0], accum_slots[0, 0], outs
        )
        across = moved(fresh, "rep", lambda i: i ^ 2)
        pieces = [fresh, moved(fresh, "rep", lambda i: i ^ 1), across, moved(across, "rep", lambda i: i ^ 1)]
        working_next = place(
            shards, pieces, drs[0] * FIELD * geo[3], weights.shape, working_next
        )
    master_next, accum_next = outs
    return (working_next[None], master_next[None, None], accum_next[None, None])


def solution(mesh):
    placed = (
        P("rep", "site", None, None, None),
        P("site", "rep", None, None, None),
        P("site", "rep", None, None, None),
        P(None, None, "site", None),
        P(None, "site", None, None, None),
        P(),
        P(),
    )
    return jax.shard_map(
        per_device,
        mesh=mesh,
        in_specs=placed,
        out_specs=(
            P("site", None, None, None),
            P("site", "rep", None, None, None),
            P("site", "rep", None, None, None),
        ),
        check_vma=False,
    )
```

time: 343 us -> 323 us (0.942)
  Pallas kernels: 0 us -> 199 us
  matrix products: 74.1 us -> 0 us
  waiting for transfers between devices: 138 us -> 85.7 us
  local copies, waits for them, and re-layouts: 50.5 us -> 8.98 us
  starting transfers between devices: 39.8 us -> 21.2 us
  between operations: 20.5 us -> 2.85 us
  other arithmetic: 17.9 us -> 5.01 us
    pallas_call x0 -> x8, Pallas kernels: none -> 199 us  [the longest x3 148 us: place(): pl.pallas_call(functools.partial(place_kernel, first_lane, block, 4), out...]
    dot_general x3 -> x0, matrix products: 74.1 us -> none  [per_device(): jnp.einsum('cob,bck->cok', signal, patches, preferred_element_type=jnp.fl...]
    reduce_scatter x1 -> x0, waiting for transfers between devices: 53.7 us -> none  [per_device(): lax.psum_scatter(ordered, 'rep', scatter_dimension=0, tiled=True)]
    ppermute x15 -> x24, waiting for transfers between devices: 46 us -> 85.7 us  [moved(): lax.ppermute(x, axis, [(i, t) for i, t in pairs if t is not None and 0 <=...]
    all_gather x1 -> x0, waiting for transfers between devices: 37.9 us -> none  [per_device(): lax.all_gather(master_next[0].astype(jnp.bfloat16), 'rep', axis=0, tiled=...]
    transpose x3 -> x0, local copies, waits for them, and re-layouts: 20.2 us -> none  [build_patches(): stacked.transpose(0, 3, 1, 2, 4)]
    ppermute x15 -> x24, starting transfers between devices: 39.7 us -> 21.2 us  [moved(): lax.ppermute(x, axis, [(i, t) for i, t in pairs if t is not None and 0 <=...]
    convert_element_type x2 -> x0, other arithmetic: 11.4 us -> none  [the longest x1 5.78 us: per_device(): master_next[0].astype(jnp.bfloat16)]
  transfers between devices with their start and end apart: 17 -> 24, of which waited for: 5 -> 8; matrix products, arithmetic and copies ran while one was open for 22% -> 3% of each run, Pallas kernels for 0% -> 38%
where the time goes in v1:
time: 323 us
  Pallas kernels  199 us (62%)
  waiting for transfers between devices  85.7 us (27%)
  starting transfers between devices  21.2 us (7%)
  local copies, waits for them, and re-layouts  8.98 us (3%)
  other arithmetic  5.01 us (2%)
    pallas_call x3, Pallas kernels, place(): pl.pallas_call(functools.partial(place_kernel, first_lane, block, 4), out...  148 us
    ppermute x24, waiting for transfers between devices, moved(): lax.ppermute(x, axis, [(i, t) for i, t in pairs if t is not None and 0 <=...  85.7 us
    pallas_call x3, Pallas kernels, backward(): pl.pallas_call(functools.partial(backward_kernel, geo, drs, len(flat), n_...  26.3 us
    pallas_call x2, Pallas kernels, forward(): pl.pallas_call(functools.partial(forward_kernel, geo, drs, last, len(flat...  24.5 us
    ppermute x24, starting transfers between devices, moved(): lax.ppermute(x, axis, [(i, t) for i, t in pairs if t is not None and 0 <=...  21.2 us
  transfers between devices with their start and end apart: 24, of which 8 were waited for; matrix products, arithmetic and copies ran while one was open for 3% of the time, Pallas kernels for 38%

profile of v1, /device:TPU:3, one launch (start us, length us, event | category | flops | bytes accessed | tf_op | source)
XLA Modules:
  0.0 322.9 jit_solution(11570558834006601555)
XLA Ops:
  1.9 4.2 %collective-permute-start.10 = (bf16[2,256,1024]{2,1,0:T(8,128)(2,1)S(1)}, bf16[2,256,1024]{2,1,0:T(8,128)(2,1)}, u32[]{:S(2)}, u32[]{:S(2)}) collective-permute-start(bf16[2,256,1024]{2,1,0:T(8,128)(2,1)S(1)} %dynamic-slice_bitcast_fusion.3), channel_id=1, source_target_pairs={{0,2},{1,3},{2,4},{3,5},{4,6},{5,7},{8,10},{9,11},{10,12},{11,13},... | collective-permute-start | bytes 3145736 | tf_op jit(solution)/shard_map/ppermute | solution.py:25
  6.1 1.5 fusion.4
  9.5 2.2 dynamic-slice_bitcast_fusion
  11.8 2.1 collective-permute-start.9
  15.6 11.4 %collective-permute-done.10.refs_3_ = bf16[2,256,1024]{2,1,0:T(8,128)(2,1)} collective-permute-done((bf16[2,256,1024]{2,1,0:T(8,128)(2,1)S(1)}, bf16[2,256,1024]{2,1,0:T(8,128)(2,1)}, u32[]{:S(2)}, u32[]{:S(2)}) %collective-permute-start.10) | collective-permute-done | bytes 1048608 | tf_op jit(solution)/shard_map/ppermute | solution.py:25
  28.2 11.0 %collective-permute-done.2.refs_7_.refs_9_.refs_3_ = bf16[2,256,1024]{2,1,0:T(8,128)(2,1)S(1)} collective-permute-done((bf16[2,256,1024]{2,1,0:T(8,128)(2,1)S(1)}, bf16[2,256,1024]{2,1,0:T(8,128)(2,1)S(1)}, u32[]{:S(2)}, u32[]{:S(2)}) %collective-permute-start.2) | collective-permute-done | bytes 1048608 | tf_op jit(solution)/shard_map/ppermute | solution.py:25
  39.5 1.5 collective-permute-done.refs_13_.refs_3_
  41.1 1.7 collective-permute-start.12
  45.3 20.6 %collective-permute-done.8.refs_17_.refs_9_ = bf16[4,64,2304]{2,1,0:T(8,128)(2,1)S(1)} collective-permute-done((bf16[4,64,2304]{2,1,0:T(8,128)(2,1)S(1)}, bf16[4,64,2304]{2,1,0:T(8,128)(2,1)S(1)}, u32[]{:S(2)}, u32[]{:S(2)}) %collective-permute-start.8) | collective-permute-done | bytes 1179680 | tf_op jit(solution)/shard_map/ppermute | solution.py:25
  66.9 1.8 collective-permute-done.3.refs_11_.refs_3_.refs_5_
  68.6 1.5 collective-permute-start.4
  70.2 23.3 %collective-permute-done.5.refs_5_.refs_7_ = bf16[2,256,1024]{2,1,0:T(8,128)(2,1)} collective-permute-done((bf16[2,256,1024]{2,1,0:T(8,128)(2,1)}, bf16[2,256,1024]{2,1,0:T(8,128)(2,1)}, u32[]{:S(2)}, u32[]{:S(2)}) %collective-permute-start.5) | collective-permute-done | bytes 1048608 | tf_op jit(solution)/shard_map/ppermute | solution.py:25
  93.4 1.8 collective-permute-start.6
  98.1 15.6 %forward.2.refs_11_ = f32[12,256,256]{2,1,0:T(8,128)} custom-call(s32[3]{0:T(128)} %pad_add_fusion.1.refs_0_, s32[12]{0:T(128)} %pad_add_fusion.2.refs_1_, bf16[4,256,1024]{2,1,0:T(8,128)(2,1)} %bitcast.29, bf16[2,256,1024]{2,1,0:T(8,128)(2,1)} %collective-permute-done.10.refs_3_, bf16[2,256,1024]{2,1,0:T(8,128)(2,1)} %copy-done.6, ...), custom_call_target="tpu_custom_call" | custom-call | flops 5033164800 | bytes 8388608 | tf_op jit(solution)/shard_map/forward/pallas_call | solution.py:268
  113.7 8.9 %forward.3.refs_9_.refs_7_ = bf16[12,256,256]{2,1,0:T(8,128)(2,1)} custom-call(s32[3]{0:T(128)} %pad_add_fusion.1.refs_0_, s32[12]{0:T(128)} %pad_add_fusion.2.refs_1_, bf16[4,256,1024]{2,1,0:T(8,128)(2,1)} %bitcast.30, bf16[2,256,1024]{2,1,0:T(8,128)(2,1)} %copy-done.2, bf16[2,256,1024]{2,1,0:T(8,128)(2,1)} %collective-permute-done.4.refs_12_.refs_4_.refs_6_, ...), custom_call_target="tpu_custom_call" | custom-call | flops 1006632960 | bytes 8388608 | tf_op jit(solution)/shard_map/forward/pallas_call | solution.py:268
  122.7 8.7 %backward.3 = (bf16[4,64,768]{2,1,0:T(8,128)(2,1)}, f32[4,64,2304]{2,1,0:T(8,128)}, f32[4,64,2304]{2,1,0:T(8,128)}) custom-call(s32[3]{0:T(128)} %pad_add_fusion.1.refs_0_, s32[12]{0:T(128)} %pad_add_fusion.2.refs_1_, bf16[4,256,1024]{2,1,0:T(8,128)(2,1)} %bitcast.31, bf16[2,256,1024]{2,1,0:T(8,128)(2,1)} %collective-permute-done.10.refs_3_, ...), custom_call_target="tpu_custom_call" | custom-call | flops 2013265920 | bytes 8388608 | tf_op jit(solution)/shard_map/backward/pallas_call | solution.py:295
  131.4 8.8 %backward.4 = (bf16[4,64,768]{2,1,0:T(8,128)(2,1)}, f32[4,64,2304]{2,1,0:T(8,128)}, f32[4,64,2304]{2,1,0:T(8,128)}) custom-call(s32[3]{0:T(128)} %pad_add_fusion.1.refs_0_, s32[12]{0:T(128)} %pad_add_fusion.2.refs_1_, bf16[4,256,1024]{2,1,0:T(8,128)(2,1)} %bitcast.32, bf16[2,256,1024]{2,1,0:T(8,128)(2,1)} %copy-done, ...), custom_call_target="tpu_custom_call", output_to_operand_aliasing={{1}: (10, {}), {2}: (11, {})} | custom-call | flops 2013265920 | bytes 8388608 | tf_op jit(solution)/shard_map/backward/pallas_call | solution.py:295
  141.7 8.8 %backward.5 = (bf16[4,64,768]{2,1,0:T(8,128)(2,1)}, f32[4,64,2304]{2,1,0:T(8,128)}, f32[4,64,2304]{2,1,0:T(8,128)}) custom-call(s32[3]{0:T(128)} %pad_add_fusion.1.refs_0_, s32[12]{0:T(128)} %pad_add_fusion.2.refs_1_, bf16[4,256,1024]{2,1,0:T(8,128)(2,1)} %bitcast.33, ...), custom_call_target="tpu_custom_call", output_to_operand_aliasing={{1}: (12, {}), {2}: (13, {})} | custom-call | flops 2013265920 | bytes 8388608 | tf_op jit(solution)/shard_map/backward/pallas_call | solution.py:295
  151.1 8.9 %collective-permute-done.22.refs_3_ = bf16[4,64,768]{2,1,0:T(8,128)(2,1)S(1)} collective-permute-done((bf16[4,64,768]{2,1,0:T(8,128)(2,1)S(1)}, bf16[4,64,768]{2,1,0:T(8,128)(2,1)S(1)}, u32[]{:S(2)}, u32[]{:S(2)}) %collective-permute-start.22) | collective-permute-done | bytes 393248 | tf_op jit(solution)/shard_map/ppermute | solution.py:25
  160.5 7.3 %collective-permute-done.16.refs_3_ = bf16[4,64,768]{2,1,0:T(8,128)(2,1)S(1)} collective-permute-done((bf16[4,64,768]{2,1,0:T(8,128)(2,1)}, bf16[4,64,768]{2,1,0:T(8,128)(2,1)S(1)}, u32[]{:S(2)}, u32[]{:S(2)}) %collective-permute-start.16) | collective-permute-done | bytes 393248 | tf_op jit(solution)/shard_map/ppermute | solution.py:25
  168.3 3.2 pad_add_fusion.refs_0_
  171.5 49.4 %place.3.refs_5_ = bf16[16,64,2304]{2,1,0:T(8,128)(2,1)} custom-call(s32[4]{0:T(128)} %pad_add_fusion.refs_0_, bf16[4,64,768]{2,1,0:T(8,128)(2,1)} %get-tuple-element.18.refs_1_, bf16[4,64,768]{2,1,0:T(8,128)(2,1)} %collective-permute-done.21.refs_2_, bf16[4,64,768]{2,1,0:T(8,128)(2,1)} %copy-done.15, bf16[4,64,768]{2,1,0:T(8,128)(2,1)} %collective-permute-done.23.refs_4_), custom_call_target="tpu_custom_call" | custom-call | tf_op jit(solution)/shard_map/place/pallas_call | solution.py:346
  222.4 49.4 %place.4.refs_5_ = bf16[16,64,2304]{2,1,0:T(8,128)(2,1)} custom-call(s32[4]{0:T(128)} %pad_add_fusion.refs_0_, bf16[4,64,768]{2,1,0:T(8,128)(2,1)} %get-tuple-element.17.refs_1_, bf16[4,64,768]{2,1,0:T(8,128)(2,1)} %copy-done.10, bf16[4,64,768]{2,1,0:T(8,128)(2,1)} %copy-done.8, bf16[4,64,768]{2,1,0:T(8,128)(2,1)} %copy-done.12, ...), custom_call_target="tpu_custom_call", output_to_operand_aliasing={{}: (5, {})} | custom-call | tf_op jit(solution)/shard_map/place/pallas_call | solution.py:346
  273.4 49.4 %place.5 = bf16[16,64,2304]{2,1,0:T(8,128)(2,1)} custom-call(s32[4]{0:T(128)} %pad_add_fusion.refs_0_, bf16[4,64,768]{2,1,0:T(8,128)(2,1)} %get-tuple-element.16.refs_1_, bf16[4,64,768]{2,1,0:T(8,128)(2,1)} %copy-done.11, bf16[4,64,768]{2,1,0:T(8,128)(2,1)} %copy-done.9, bf16[4,64,768]{2,1,0:T(8,128)(2,1)} %copy-done.13, ...), custom_call_target="tpu_custom_call", output_to_operand_aliasing={{}: (5, {})} | custom-call | tf_op jit(solution)/shard_map/place/pallas_call | solution.py:346
  (73 shorter events, 17.0 us)
Async XLA Ops:
  1.9 25.0 %collective-permute-start.10 = (bf16[2,256,1024]{2,1,0:T(8,128)(2,1)S(1)}, bf16[2,256,1024]{2,1,0:T(8,128)(2,1)}, u32[]{:S(2)}, u32[]{:S(2)}) collective-permute-start(bf16[2,256,1024]{2,1,0:T(8,128)(2,1)S(1)} %dynamic-slice_bitcast_fusion.3), channel_id=1, source_target_pairs={{0,2},{1,3},{2,4},{3,5},{4,6},{5,7},{8,10},{9,11},{10,12},{11,13},... | collective-permute-start | bytes 3145736 | tf_op jit(solution)/shard_map/ppermute | solution.py:25
  11.8 30.9 %collective-permute-start.9 = (bf16[4,64,2304]{2,1,0:T(8,128)(2,1)S(1)}, bf16[4,64,2304]{2,1,0:T(8,128)(2,1)S(1)}, u32[]{:S(2)}, u32[]{:S(2)}) collective-permute-start(bf16[4,64,2304]{2,1,0:T(8,128)(2,1)S(1)} %get-tuple-element.21), channel_id=1, source_target_pairs={{0,24},{8,16},{16,8},{24,0},{1,25},{9,17},{17,9},{25,1},{2,26},{10... | collective-permute-start | bytes 3538952 | tf_op jit(solution)/shard_map/ppermute | solution.py:25
  13.9 25.3 %collective-permute-start.2 = (bf16[2,256,1024]{2,1,0:T(8,128)(2,1)S(1)}, bf16[2,256,1024]{2,1,0:T(8,128)(2,1)S(1)}, u32[]{:S(2)}, u32[]{:S(2)}) collective-permute-start(bf16[2,256,1024]{2,1,0:T(8,128)(2,1)S(1)} %dynamic-slice_bitcast_fusion.3), channel_id=1, source_target_pairs={{0,1},{1,0},{2,3},{3,2},{4,5},{5,4},{6,7},{7,6},{8,9},{9,8},{10,11... | collective-permute-start | bytes 3145736 | tf_op jit(solution)/shard_map/ppermute | solution.py:25
  14.2 26.9 %collective-permute-start = (bf16[2,256,1024]{2,1,0:T(8,128)(2,1)S(1)}, bf16[2,256,1024]{2,1,0:T(8,128)(2,1)}, u32[]{:S(2)}, u32[]{:S(2)}) collective-permute-start(bf16[2,256,1024]{2,1,0:T(8,128)(2,1)S(1)} %dynamic-slice_bitcast_fusion.3), channel_id=1, source_target_pairs={{2,0},{3,1},{4,2},{5,3},{6,4},{7,5},{10,8},{11,9},{12,10},{13,11},... | collective-permute-start | bytes 3145736 | tf_op jit(solution)/shard_map/ppermute | solution.py:25
  15.5 28.5 %collective-permute-start.7 = (bf16[4,64,2304]{2,1,0:T(8,128)(2,1)S(1)}, bf16[4,64,2304]{2,1,0:T(8,128)(2,1)S(1)}, u32[]{:S(2)}, u32[]{:S(2)}) collective-permute-start(bf16[4,64,2304]{2,1,0:T(8,128)(2,1)S(1)} %get-tuple-element.22), channel_id=1, source_target_pairs={{0,8},{8,0},{16,24},{24,16},{1,9},{9,1},{17,25},{25,17},{2,10},{10... | collective-permute-start | bytes 3538952 | tf_op jit(solution)/shard_map/ppermute | solution.py:25
  27.0 38.9 %collective-permute-start.8 = (bf16[4,64,2304]{2,1,0:T(8,128)(2,1)S(1)}, bf16[4,64,2304]{2,1,0:T(8,128)(2,1)S(1)}, u32[]{:S(2)}, u32[]{:S(2)}) collective-permute-start(bf16[4,64,2304]{2,1,0:T(8,128)(2,1)S(1)} %get-tuple-element.23), channel_id=1, source_target_pairs={{0,16},{8,24},{16,0},{24,8},{1,17},{9,25},{17,1},{25,9},{2,18},{10... | collective-permute-start | bytes 3538952 | tf_op jit(solution)/shard_map/ppermute | solution.py:25
  39.2 27.2 %collective-permute-start.11 = (bf16[2,256,1024]{2,1,0:T(8,128)(2,1)}, bf16[2,256,1024]{2,1,0:T(8,128)(2,1)S(1)}, u32[]{:S(2)}, u32[]{:S(2)}) collective-permute-start(bf16[2,256,1024]{2,1,0:T(8,128)(2,1)} %collective-permute-done.10.refs_3_), channel_id=1, source_target_pairs={{0,8},{8,0},{16,24},{24,16},{1,9},{9,1},{17,25},{25,17},{2,10},{10... | collective-permute-start | bytes 3145736 | tf_op jit(solution)/shard_map/ppermute | solution.py:25
  41.1 25.4 %collective-permute-start.12 = (bf16[2,256,1024]{2,1,0:T(8,128)(2,1)S(1)}, bf16[2,256,1024]{2,1,0:T(8,128)(2,1)}, u32[]{:S(2)}, u32[]{:S(2)}) collective-permute-start(bf16[2,256,1024]{2,1,0:T(8,128)(2,1)S(1)} %collective-permute-done.2.refs_7_.refs_9_.refs_3_), channel_id=1, source_target_pairs={{0,2},{2,4},{4,6},{8,10},{10,12},{12,14},{16,18},{18,20},{20,22},{... | collective-permute-start | bytes 3145736 | tf_op jit(solution)/shard_map/ppermute | solution.py:25
  42.7 25.9 %collective-permute-start.3 = (bf16[2,256,1024]{2,1,0:T(8,128)(2,1)S(1)}, bf16[2,256,1024]{2,1,0:T(8,128)(2,1)S(1)}, u32[]{:S(2)}, u32[]{:S(2)}) collective-permute-start(bf16[2,256,1024]{2,1,0:T(8,128)(2,1)S(1)} %collective-permute-done.2.refs_7_.refs_9_.refs_3_), channel_id=1, source_target_pairs={{2,0},{3,1},{4,2},{5,3},{6,4},{7,5},{10,8},{11,9},{12,10},{13,11},... | collective-permute-start | bytes 3145736 | tf_op jit(solution)/shard_map/ppermute | solution.py:25
  44.0 49.4 %collective-permute-start.5 = (bf16[2,256,1024]{2,1,0:T(8,128)(2,1)}, bf16[2,256,1024]{2,1,0:T(8,128)(2,1)}, u32[]{:S(2)}, u32[]{:S(2)}) collective-permute-start(bf16[2,256,1024]{2,1,0:T(8,128)(2,1)} %collective-permute-done.refs_13_.refs_3_), channel_id=1, source_target_pairs={{2,1},{4,3},{6,5},{10,9},{12,11},{14,13},{18,17},{20,19},{22,21},{... | collective-permute-start | bytes 3145736 | tf_op jit(solution)/shard_map/ppermute | solution.py:25
  65.9 31.3 %collective-permute-start.14 = (bf16[2,256,1024]{2,1,0:T(8,128)(2,1)S(1)}, bf16[2,256,1024]{2,1,0:T(8,128)(2,1)S(1)}, u32[]{:S(2)}, u32[]{:S(2)}) collective-permute-start(bf16[2,256,1024]{2,1,0:T(8,128)(2,1)S(1)} %collective-permute-done.2.refs_7_.refs_9_.refs_3_), channel_id=1, source_target_pairs={{0,8},{8,0},{16,24},{24,16},{1,9},{9,1},{17,25},{25,17},{2,10},{10... | collective-permute-start | bytes 3145736 | tf_op jit(solution)/shard_map/ppermute | solution.py:25
  66.4 30.8 %collective-permute-start.1 = (bf16[2,256,1024]{2,1,0:T(8,128)(2,1)}, bf16[2,256,1024]{2,1,0:T(8,128)(2,1)}, u32[]{:S(2)}, u32[]{:S(2)}) collective-permute-start(bf16[2,256,1024]{2,1,0:T(8,128)(2,1)} %collective-permute-done.refs_13_.refs_3_), channel_id=1, source_target_pairs={{0,8},{8,0},{16,24},{24,16},{1,9},{9,1},{17,25},{25,17},{2,10},{10... | collective-permute-start | bytes 3145736 | tf_op jit(solution)/shard_map/ppermute | solution.py:25
  66.4 30.7 %collective-permute-start.13 = (bf16[2,256,1024]{2,1,0:T(8,128)(2,1)}, bf16[2,256,1024]{2,1,0:T(8,128)(2,1)}, u32[]{:S(2)}, u32[]{:S(2)}) collective-permute-start(bf16[2,256,1024]{2,1,0:T(8,128)(2,1)} %collective-permute-done.12.refs_5_), channel_id=1, source_target_pairs={{0,8},{8,0},{16,24},{24,16},{1,9},{9,1},{17,25},{25,17},{2,10},{10... | collective-permute-start | bytes 3145736 | tf_op jit(solution)/shard_map/ppermute | solution.py:25
  68.6 28.5 %collective-permute-start.4 = (bf16[2,256,1024]{2,1,0:T(8,128)(2,1)S(1)}, bf16[2,256,1024]{2,1,0:T(8,128)(2,1)}, u32[]{:S(2)}, u32[]{:S(2)}) collective-permute-start(bf16[2,256,1024]{2,1,0:T(8,128)(2,1)S(1)} %collective-permute-done.3.refs_11_.refs_3_.refs_5_), channel_id=1, source_target_pairs={{0,8},{8,0},{16,24},{24,16},{1,9},{9,1},{17,25},{25,17},{2,10},{10... | collective-permute-start | bytes 3145736 | tf_op jit(solution)/shard_map/ppermute | solution.py:25
  93.4 20.3 %collective-permute-start.6 = (bf16[2,256,1024]{2,1,0:T(8,128)(2,1)}, bf16[2,256,1024]{2,1,0:T(8,128)(2,1)}, u32[]{:S(2)}, u32[]{:S(2)}) collective-permute-start(bf16[2,256,1024]{2,1,0:T(8,128)(2,1)} %collective-permute-done.5.refs_5_.refs_7_), channel_id=1, source_target_pairs={{0,8},{8,0},{16,24},{24,16},{1,9},{9,1},{17,25},{25,17},{2,10},{10... | collective-permute-start | bytes 3145736 | tf_op jit(solution)/shard_map/ppermute | solution.py:25
  140.2 19.8 %collective-permute-start.19 = (bf16[4,64,768]{2,1,0:T(8,128)(2,1)}, bf16[4,64,768]{2,1,0:T(8,128)(2,1)S(1)}, u32[]{:S(2)}, u32[]{:S(2)}) collective-permute-start(bf16[4,64,768]{2,1,0:T(8,128)(2,1)} %get-tuple-element.17.refs_1_), channel_id=1, source_target_pairs={{0,16},{8,24},{16,0},{24,8},{1,17},{9,25},{17,1},{25,9},{2,18},{10... | collective-permute-start | bytes 1179656 | tf_op jit(solution)/shard_map/ppermute | solution.py:25
  140.3 19.7 %collective-permute-start.22 = (bf16[4,64,768]{2,1,0:T(8,128)(2,1)S(1)}, bf16[4,64,768]{2,1,0:T(8,128)(2,1)S(1)}, u32[]{:S(2)}, u32[]{:S(2)}) collective-permute-start(bf16[4,64,768]{2,1,0:T(8,128)(2,1)S(1)} %copy-done.14), channel_id=1, source_target_pairs={{0,16},{8,24},{16,0},{24,8},{1,17},{9,25},{17,1},{25,9},{2,18},{10... | collective-permute-start | bytes 1179656 | tf_op jit(solution)/shard_map/ppermute | solution.py:25
  150.5 17.3 %collective-permute-start.16 = (bf16[4,64,768]{2,1,0:T(8,128)(2,1)}, bf16[4,64,768]{2,1,0:T(8,128)(2,1)S(1)}, u32[]{:S(2)}, u32[]{:S(2)}) collective-permute-start(bf16[4,64,768]{2,1,0:T(8,128)(2,1)} %get-tuple-element.16.refs_1_), channel_id=1, source_target_pairs={{0,16},{8,24},{16,0},{24,8},{1,17},{9,25},{17,1},{25,9},{2,18},{10... | collective-permute-start | bytes 1179656 | tf_op jit(solution)/shard_map/ppermute | solution.py:25
  150.6 17.5 %collective-permute-start.21 = (bf16[4,64,768]{2,1,0:T(8,128)(2,1)S(1)}, bf16[4,64,768]{2,1,0:T(8,128)(2,1)}, u32[]{:S(2)}, u32[]{:S(2)}) collective-permute-start(bf16[4,64,768]{2,1,0:T(8,128)(2,1)S(1)} %copy-done.14), channel_id=1, source_target_pairs={{0,8},{8,0},{16,24},{24,16},{1,9},{9,1},{17,25},{25,17},{2,10},{10... | collective-permute-start | bytes 1179656 | tf_op jit(solution)/shard_map/ppermute | solution.py:25
  150.7 70.3 %collective-permute-start.18 = (bf16[4,64,768]{2,1,0:T(8,128)(2,1)S(1)}, bf16[4,64,768]{2,1,0:T(8,128)(2,1)S(1)}, u32[]{:S(2)}, u32[]{:S(2)}) collective-permute-start(bf16[4,64,768]{2,1,0:T(8,128)(2,1)S(1)} %copy-done.7), channel_id=1, source_target_pairs={{0,8},{8,0},{16,24},{24,16},{1,9},{9,1},{17,25},{25,17},{2,10},{10... | collective-permute-start | bytes 1179656 | tf_op jit(solution)/shard_map/ppermute | solution.py:25
  160.0 11.4 %collective-permute-start.23 = (bf16[4,64,768]{2,1,0:T(8,128)(2,1)S(1)}, bf16[4,64,768]{2,1,0:T(8,128)(2,1)}, u32[]{:S(2)}, u32[]{:S(2)}) collective-permute-start(bf16[4,64,768]{2,1,0:T(8,128)(2,1)S(1)} %collective-permute-done.22.refs_3_), channel_id=1, source_target_pairs={{0,8},{8,0},{16,24},{24,16},{1,9},{9,1},{17,25},{25,17},{2,10},{10... | collective-permute-start | bytes 1179656 | tf_op jit(solution)/shard_map/ppermute | solution.py:25
  160.0 60.9 %collective-permute-start.20 = (bf16[4,64,768]{2,1,0:T(8,128)(2,1)S(1)}, bf16[4,64,768]{2,1,0:T(8,128)(2,1)S(1)}, u32[]{:S(2)}, u32[]{:S(2)}) collective-permute-start(bf16[4,64,768]{2,1,0:T(8,128)(2,1)S(1)} %collective-permute-done.19.refs_3_), channel_id=1, source_target_pairs={{0,8},{8,0},{16,24},{24,16},{1,9},{9,1},{17,25},{25,17},{2,10},{10... | collective-permute-start | bytes 1179656 | tf_op jit(solution)/shard_map/ppermute | solution.py:25
  167.8 104.1 %collective-permute-start.15 = (bf16[4,64,768]{2,1,0:T(8,128)(2,1)}, bf16[4,64,768]{2,1,0:T(8,128)(2,1)S(1)}, u32[]{:S(2)}, u32[]{:S(2)}) collective-permute-start(bf16[4,64,768]{2,1,0:T(8,128)(2,1)} %get-tuple-element.16.refs_1_), channel_id=1, source_target_pairs={{0,8},{8,0},{16,24},{24,16},{1,9},{9,1},{17,25},{25,17},{2,10},{10... | collective-permute-start | bytes 1179656 | tf_op jit(solution)/shard_map/ppermute | solution.py:25
  168.1 103.8 %collective-permute-start.17 = (bf16[4,64,768]{2,1,0:T(8,128)(2,1)S(1)}, bf16[4,64,768]{2,1,0:T(8,128)(2,1)S(1)}, u32[]{:S(2)}, u32[]{:S(2)}) collective-permute-start(bf16[4,64,768]{2,1,0:T(8,128)(2,1)S(1)} %collective-permute-done.16.refs_3_), channel_id=1, source_target_pairs={{0,8},{8,0},{16,24},{24,16},{1,9},{9,1},{17,25},{25,17},{2,10},{10... | collective-permute-start | bytes 1179656 | tf_op jit(solution)/shard_map/ppermute | solution.py:25
  (17 other events, 427.5 us)

commit v2 on v1

--- a/solution.py
+++ b/solution.py
@@ -323,33 +323,41 @@
     )(info, choice, own, *flat, sig, master, accum, *(outs or ()))
 
 
-def place_kernel(first_lane, block, shards, *refs):
+def place_kernel(first_lane, block, *refs):
     a = refs[1:5]
-    out, sem = refs[-2:]
-    copies = [
+    out, held, in_sem, out_sem = refs[-4:]
+    takes = [pltpu.make_async_copy(a[k], held.at[k], in_sem.at[k]) for k in range(4)]
+    puts = [
         pltpu.make_async_copy(
-            a[k],
+            held.at[k],
             out.at[pl.ds(refs[0][k] * block, block), :, pl.ds(first_lane, a[k].shape[2])],
-            sem.at[k],
+            out_sem.at[k],
         )
         for k in range(4)
     ]
-    for c in copies:
-        c.start()
-    for c in copies:
-        c.wait()
+    for take in takes:
+        take.start()
+    for take, put in zip(takes, puts):
+        take.wait()
+        put.start()
+    for put in puts:
+        put.wait()
 
 
 def place(shards, pieces, first_lane, shape, out):
     block = pieces[0].shape[0]
     extra = [] if out is None else [out]
     return pl.pallas_call(
-        functools.partial(place_kernel, first_lane, block, 4),
+        functools.partial(place_kernel, first_lane, block),
         out_shape=jax.ShapeDtypeStruct(shape, jnp.bfloat16),
         in_specs=[SMEM] + [ANY] * (4 + len(extra)),
         out_specs=ANY,
         input_output_aliases={5: 0} if extra else {},
-        scratch_shapes=[pltpu.SemaphoreType.DMA((4,))],
+        scratch_shapes=[
+            pltpu.VMEM((4,) + pieces[0].shape, jnp.bfloat16),
+            pltpu.SemaphoreType.DMA((4,)),
+            pltpu.SemaphoreType.DMA((4,)),
+        ],
         name="place",
     )(shards, *pieces, *extra)
 

time: 323 us -> 184 us (0.57)
  Pallas kernels: 199 us -> 57.7 us
  starting transfers between devices: 21.2 us -> 25.9 us
  waiting for transfers between devices: 85.7 us -> 82 us
    pallas_call x3, Pallas kernels: 148 us -> 8.58 us  [place(): pl.pallas_call(functools.partial(place_kernel, first_lane, block), out_sh...]
    ppermute x24, starting transfers between devices: 21.2 us -> 25.9 us  [moved(): lax.ppermute(x, axis, [(i, t) for i, t in pairs if t is not None and 0 <=...]
    ppermute x24, waiting for transfers between devices: 85.7 us -> 82 us  [moved(): lax.ppermute(x, axis, [(i, t) for i, t in pairs if t is not None and 0 <=...]
  transfers between devices with their start and end apart: 24 -> 24, of which waited for: 8 -> 8; matrix products, arithmetic and copies ran while one was open for 3% -> 5% of each run, Pallas kernels for 38% -> 16%
where the time goes in v2:
time: 184 us; the launch traced here: 182 us
  waiting for transfers between devices  82 us (45%)
  Pallas kernels  57.7 us (31%)
  starting transfers between devices  25.9 us (14%)
  local copies, waits for them, and re-layouts  8.98 us (5%)
  other arithmetic  5.01 us (3%)
  between operations  2.81 us (2%)
    ppermute x24, waiting for transfers between devices, moved(): lax.ppermute(x, axis, [(i, t) for i, t in pairs if t is not None and 0 <=...  82 us
    ppermute x24, starting transfers between devices, moved(): lax.ppermute(x, axis, [(i, t) for i, t in pairs if t is not None and 0 <=...  25.9 us
    pallas_call x3, Pallas kernels, backward(): pl.pallas_call(functools.partial(backward_kernel, geo, drs, len(flat), n_...  25.3 us
    pallas_call x2, Pallas kernels, forward(): pl.pallas_call(functools.partial(forward_kernel, geo, drs, last, len(flat...  23.8 us
    pallas_call x3, Pallas kernels, place(): pl.pallas_call(functools.partial(place_kernel, first_lane, block), out_sh...  8.58 us
    unnamed x34, local copies, waits for them, and re-layouts  3.95 us
  transfers between devices with their start and end apart: 24, of which 8 were waited for; matrix products, arithmetic and copies ran while one was open for 5% of the time, Pallas kernels for 16%

profile of v2, /device:TPU:3, one launch (start us, length us, event | category | flops | bytes accessed | tf_op | source)
XLA Modules:
  0.0 182.4 jit_solution(2033652514686109722)
XLA Ops:
  1.9 4.2 %collective-permute-start.10 = (bf16[2,256,1024]{2,1,0:T(8,128)(2,1)S(1)}, bf16[2,256,1024]{2,1,0:T(8,128)(2,1)}, u32[]{:S(2)}, u32[]{:S(2)}) collective-permute-start(bf16[2,256,1024]{2,1,0:T(8,128)(2,1)S(1)} %dynamic-slice_bitcast_fusion.3), channel_id=1, source_target_pairs={{0,2},{1,3},{2,4},{3,5},{4,6},{5,7},{8,10},{9,11},{10,12},{11,13},... | collective-permute-start | bytes 3145736 | tf_op jit(solution)/shard_map/ppermute | solution.py:25
  9.5 2.2 %dynamic-slice_bitcast_fusion = (bf16[4,64,2304]{2,1,0:T(8,128)(2,1)S(1)}, bf16[4,64,2304]{2,1,0:T(8,128)(2,1)S(1)}, bf16[4,64,2304]{2,1,0:T(8,128)(2,1)S(1)}) fusion(bf16[1,1,16,64,2304]{4,3,2,1,0:T(8,128)(2,1)} %param.7, s32[]{:T(128)S(6)} %select_n.48, s32[]{:T(128)S(6)} %select_n.46, s32[]{:T(128)S(6)} %select_n.47), kind=kLoop, calls=%fused_computation | loop fusion | bytes 7077900 | tf_op jit(solution)/shard_map/dynamic_slice | solution.py:391
  11.8 2.1 %collective-permute-start.9 = (bf16[4,64,2304]{2,1,0:T(8,128)(2,1)S(1)}, bf16[4,64,2304]{2,1,0:T(8,128)(2,1)S(1)}, u32[]{:S(2)}, u32[]{:S(2)}) collective-permute-start(bf16[4,64,2304]{2,1,0:T(8,128)(2,1)S(1)} %get-tuple-element.21), channel_id=1, source_target_pairs={{0,24},{8,16},{16,8},{24,0},{1,25},{9,17},{17,9},{25,1},{2,26},{10... | collective-permute-start | bytes 3538952 | tf_op jit(solution)/shard_map/ppermute | solution.py:25
  15.6 11.4 %collective-permute-done.10.refs_3_ = bf16[2,256,1024]{2,1,0:T(8,128)(2,1)} collective-permute-done((bf16[2,256,1024]{2,1,0:T(8,128)(2,1)S(1)}, bf16[2,256,1024]{2,1,0:T(8,128)(2,1)}, u32[]{:S(2)}, u32[]{:S(2)}) %collective-permute-start.10) | collective-permute-done | bytes 1048608 | tf_op jit(solution)/shard_map/ppermute | solution.py:25
  28.2 11.0 %collective-permute-done.2.refs_7_.refs_9_.refs_3_ = bf16[2,256,1024]{2,1,0:T(8,128)(2,1)S(1)} collective-permute-done((bf16[2,256,1024]{2,1,0:T(8,128)(2,1)S(1)}, bf16[2,256,1024]{2,1,0:T(8,128)(2,1)S(1)}, u32[]{:S(2)}, u32[]{:S(2)}) %collective-permute-start.2) | collective-permute-done | bytes 1048608 | tf_op jit(solution)/shard_map/ppermute | solution.py:25
  39.5 1.5 collective-permute-done.refs_13_.refs_3_
  41.1 1.7 collective-permute-start.12
  45.3 20.6 %collective-permute-done.8.refs_17_.refs_9_ = bf16[4,64,2304]{2,1,0:T(8,128)(2,1)S(1)} collective-permute-done((bf16[4,64,2304]{2,1,0:T(8,128)(2,1)S(1)}, bf16[4,64,2304]{2,1,0:T(8,128)(2,1)S(1)}, u32[]{:S(2)}, u32[]{:S(2)}) %collective-permute-start.8) | collective-permute-done | bytes 1179680 | tf_op jit(solution)/shard_map/ppermute | solution.py:25
  66.9 1.8 collective-permute-done.3.refs_11_.refs_3_.refs_5_
  70.2 23.3 %collective-permute-done.5.refs_5_.refs_7_ = bf16[2,256,1024]{2,1,0:T(8,128)(2,1)} collective-permute-done((bf16[2,256,1024]{2,1,0:T(8,128)(2,1)}, bf16[2,256,1024]{2,1,0:T(8,128)(2,1)}, u32[]{:S(2)}, u32[]{:S(2)}) %collective-permute-start.5) | collective-permute-done | bytes 1048608 | tf_op jit(solution)/shard_map/ppermute | solution.py:25
  93.4 1.8 %collective-permute-start.6 = (bf16[2,256,1024]{2,1,0:T(8,128)(2,1)}, bf16[2,256,1024]{2,1,0:T(8,128)(2,1)}, u32[]{:S(2)}, u32[]{:S(2)}) collective-permute-start(bf16[2,256,1024]{2,1,0:T(8,128)(2,1)} %collective-permute-done.5.refs_5_.refs_7_), channel_id=1, source_target_pairs={{0,8},{8,0},{16,24},{24,16},{1,9},{9,1},{17,25},{25,17},{2,10},{10... | collective-permute-start | bytes 3145736 | tf_op jit(solution)/shard_map/ppermute | solution.py:25
  98.1 15.0 %forward.2.refs_11_ = f32[12,256,256]{2,1,0:T(8,128)} custom-call(s32[3]{0:T(128)} %pad_add_fusion.1.refs_0_, s32[12]{0:T(128)} %pad_add_fusion.2.refs_1_, bf16[4,256,1024]{2,1,0:T(8,128)(2,1)} %bitcast.29, bf16[2,256,1024]{2,1,0:T(8,128)(2,1)} %collective-permute-done.10.refs_3_, bf16[2,256,1024]{2,1,0:T(8,128)(2,1)} %copy-done.6, ...), custom_call_target="tpu_custom_call" | custom-call | flops 5033164800 | bytes 8388608 | tf_op jit(solution)/shard_map/forward/pallas_call | solution.py:268
  113.1 8.8 %forward.3.refs_9_.refs_7_ = bf16[12,256,256]{2,1,0:T(8,128)(2,1)} custom-call(s32[3]{0:T(128)} %pad_add_fusion.1.refs_0_, s32[12]{0:T(128)} %pad_add_fusion.2.refs_1_, bf16[4,256,1024]{2,1,0:T(8,128)(2,1)} %bitcast.30, bf16[2,256,1024]{2,1,0:T(8,128)(2,1)} %copy-done.2, bf16[2,256,1024]{2,1,0:T(8,128)(2,1)} %collective-permute-done.4.refs_12_.refs_4_.refs_6_, ...), custom_call_target="tpu_custom_call" | custom-call | flops 1006632960 | bytes 8388608 | tf_op jit(solution)/shard_map/forward/pallas_call | solution.py:268
  122.0 8.4 %backward.3 = (bf16[4,64,768]{2,1,0:T(8,128)(2,1)}, f32[4,64,2304]{2,1,0:T(8,128)}, f32[4,64,2304]{2,1,0:T(8,128)}) custom-call(s32[3]{0:T(128)} %pad_add_fusion.1.refs_0_, s32[12]{0:T(128)} %pad_add_fusion.2.refs_1_, bf16[4,256,1024]{2,1,0:T(8,128)(2,1)} %bitcast.31, bf16[2,256,1024]{2,1,0:T(8,128)(2,1)} %collective-permute-done.10.refs_3_, ...), custom_call_target="tpu_custom_call" | custom-call | flops 2013265920 | bytes 8388608 | tf_op jit(solution)/shard_map/backward/pallas_call | solution.py:295
  130.4 8.4 %backward.4 = (bf16[4,64,768]{2,1,0:T(8,128)(2,1)}, f32[4,64,2304]{2,1,0:T(8,128)}, f32[4,64,2304]{2,1,0:T(8,128)}) custom-call(s32[3]{0:T(128)} %pad_add_fusion.1.refs_0_, s32[12]{0:T(128)} %pad_add_fusion.2.refs_1_, bf16[4,256,1024]{2,1,0:T(8,128)(2,1)} %bitcast.32, bf16[2,256,1024]{2,1,0:T(8,128)(2,1)} %copy-done, ...), custom_call_target="tpu_custom_call", output_to_operand_aliasing={{1}: (10, {}), {2}: (11, {})} | custom-call | flops 2013265920 | bytes 8388608 | tf_op jit(solution)/shard_map/backward/pallas_call | solution.py:295
  140.4 8.4 %backward.5 = (bf16[4,64,768]{2,1,0:T(8,128)(2,1)}, f32[4,64,2304]{2,1,0:T(8,128)}, f32[4,64,2304]{2,1,0:T(8,128)}) custom-call(s32[3]{0:T(128)} %pad_add_fusion.1.refs_0_, s32[12]{0:T(128)} %pad_add_fusion.2.refs_1_, bf16[4,256,1024]{2,1,0:T(8,128)(2,1)} %bitcast.33, ...), custom_call_target="tpu_custom_call", output_to_operand_aliasing={{1}: (12, {}), {2}: (13, {})} | custom-call | flops 2013265920 | bytes 8388608 | tf_op jit(solution)/shard_map/backward/pallas_call | solution.py:295
  148.8 1.6 collective-permute-start.16
  151.2 6.4 %collective-permute-done.22.refs_3_ = bf16[4,64,768]{2,1,0:T(8,128)(2,1)S(1)} collective-permute-done((bf16[4,64,768]{2,1,0:T(8,128)(2,1)S(1)}, bf16[4,64,768]{2,1,0:T(8,128)(2,1)S(1)}, u32[]{:S(2)}, u32[]{:S(2)}) %collective-permute-start.22) | collective-permute-done | bytes 393248 | tf_op jit(solution)/shard_map/ppermute | solution.py:25
  157.7 2.4 %collective-permute-start.23 = (bf16[4,64,768]{2,1,0:T(8,128)(2,1)S(1)}, bf16[4,64,768]{2,1,0:T(8,128)(2,1)}, u32[]{:S(2)}, u32[]{:S(2)}) collective-permute-start(bf16[4,64,768]{2,1,0:T(8,128)(2,1)S(1)} %collective-permute-done.22.refs_3_), channel_id=1, source_target_pairs={{0,8},{8,0},{16,24},{24,16},{1,9},{9,1},{17,25},{25,17},{2,10},{10... | collective-permute-start | bytes 1179656 | tf_op jit(solution)/shard_map/ppermute | solution.py:25
  160.1 6.0 %collective-permute-done.16.refs_3_ = bf16[4,64,768]{2,1,0:T(8,128)(2,1)S(1)} collective-permute-done((bf16[4,64,768]{2,1,0:T(8,128)(2,1)}, bf16[4,64,768]{2,1,0:T(8,128)(2,1)S(1)}, u32[]{:S(2)}, u32[]{:S(2)}) %collective-permute-start.16) | collective-permute-done | bytes 393248 | tf_op jit(solution)/shard_map/ppermute | solution.py:25
  167.6 3.2 %pad_add_fusion.refs_0_ = s32[4]{0:T(128)} fusion(s32[1]{0:T(128)} %get-tuple-element.30, s32[1]{0:T(128)} %get-tuple-element.31, s32[1]{0:T(128)} %get-tuple-element.29, s32[1]{0:T(128)} %get-tuple-element.28), kind=kLoop, calls=%fused_computation.12 | loop fusion | flops 12 | bytes 32 | tf_op jit(solution)/shard_map/stack | solution.py:380
  170.7 2.9 %place.3.refs_5_ = bf16[16,64,2304]{2,1,0:T(8,128)(2,1)} custom-call(s32[4]{0:T(128)} %pad_add_fusion.refs_0_, bf16[4,64,768]{2,1,0:T(8,128)(2,1)} %get-tuple-element.18.refs_1_, bf16[4,64,768]{2,1,0:T(8,128)(2,1)} %collective-permute-done.21.refs_2_, bf16[4,64,768]{2,1,0:T(8,128)(2,1)} %copy-done.15, bf16[4,64,768]{2,1,0:T(8,128)(2,1)} %collective-permute-done.23.refs_4_), custom_call_target="tpu_custom_call" | custom-call | tf_op jit(solution)/shard_map/place/pallas_call | solution.py:350
  175.1 2.9 %place.4.refs_5_ = bf16[16,64,2304]{2,1,0:T(8,128)(2,1)} custom-call(s32[4]{0:T(128)} %pad_add_fusion.refs_0_, bf16[4,64,768]{2,1,0:T(8,128)(2,1)} %get-tuple-element.17.refs_1_, bf16[4,64,768]{2,1,0:T(8,128)(2,1)} %copy-done.10, bf16[4,64,768]{2,1,0:T(8,128)(2,1)} %copy-done.8, bf16[4,64,768]{2,1,0:T(8,128)(2,1)} %copy-done.12, ...), custom_call_target="tpu_custom_call", output_to_operand_aliasing={{}: (5, {})} | custom-call | tf_op jit(solution)/shard_map/place/pallas_call | solution.py:350
  179.5 2.9 %place.5 = bf16[16,64,2304]{2,1,0:T(8,128)(2,1)} custom-call(s32[4]{0:T(128)} %pad_add_fusion.refs_0_, bf16[4,64,768]{2,1,0:T(8,128)(2,1)} %get-tuple-element.16.refs_1_, bf16[4,64,768]{2,1,0:T(8,128)(2,1)} %copy-done.11, bf16[4,64,768]{2,1,0:T(8,128)(2,1)} %copy-done.9, bf16[4,64,768]{2,1,0:T(8,128)(2,1)} %copy-done.13, ...), custom_call_target="tpu_custom_call", output_to_operand_aliasing={{}: (5, {})} | custom-call | tf_op jit(solution)/shard_map/place/pallas_call | solution.py:350
  (73 shorter events, 20.8 us)
Async XLA Ops:
  1.9 25.0 %collective-permute-start.10 = (bf16[2,256,1024]{2,1,0:T(8,128)(2,1)S(1)}, bf16[2,256,1024]{2,1,0:T(8,128)(2,1)}, u32[]{:S(2)}, u32[]{:S(2)}) collective-permute-start(bf16[2,256,1024]{2,1,0:T(8,128)(2,1)S(1)} %dynamic-slice_bitcast_fusion.3), channel_id=1, source_target_pairs={{0,2},{1,3},{2,4},{3,5},{4,6},{5,7},{8,10},{9,11},{10,12},{11,13},... | collective-permute-start | bytes 3145736 | tf_op jit(solution)/shard_map/ppermute | solution.py:25
  11.8 30.9 %collective-permute-start.9 = (bf16[4,64,2304]{2,1,0:T(8,128)(2,1)S(1)}, bf16[4,64,2304]{2,1,0:T(8,128)(2,1)S(1)}, u32[]{:S(2)}, u32[]{:S(2)}) collective-permute-start(bf16[4,64,2304]{2,1,0:T(8,128)(2,1)S(1)} %get-tuple-element.21), channel_id=1, source_target_pairs={{0,24},{8,16},{16,8},{24,0},{1,25},{9,17},{17,9},{25,1},{2,26},{10... | collective-permute-start | bytes 3538952 | tf_op jit(solution)/shard_map/ppermute | solution.py:25
  13.9 25.3 %collective-permute-start.2 = (bf16[2,256,1024]{2,1,0:T(8,128)(2,1)S(1)}, bf16[2,256,1024]{2,1,0:T(8,128)(2,1)S(1)}, u32[]{:S(2)}, u32[]{:S(2)}) collective-permute-start(bf16[2,256,1024]{2,1,0:T(8,128)(2,1)S(1)} %dynamic-slice_bitcast_fusion.3), channel_id=1, source_target_pairs={{0,1},{1,0},{2,3},{3,2},{4,5},{5,4},{6,7},{7,6},{8,9},{9,8},{10,11... | collective-permute-start | bytes 3145736 | tf_op jit(solution)/shard_map/ppermute | solution.py:25
  14.2 26.9 %collective-permute-start = (bf16[2,256,1024]{2,1,0:T(8,128)(2,1)S(1)}, bf16[2,256,1024]{2,1,0:T(8,128)(2,1)}, u32[]{:S(2)}, u32[]{:S(2)}) collective-permute-start(bf16[2,256,1024]{2,1,0:T(8,128)(2,1)S(1)} %dynamic-slice_bitcast_fusion.3), channel_id=1, source_target_pairs={{2,0},{3,1},{4,2},{5,3},{6,4},{7,5},{10,8},{11,9},{12,10},{13,11},... | collective-permute-start | bytes 3145736 | tf_op jit(solution)/shard_map/ppermute | solution.py:25
  15.5 28.5 %collective-permute-start.7 = (bf16[4,64,2304]{2,1,0:T(8,128)(2,1)S(1)}, bf16[4,64,2304]{2,1,0:T(8,128)(2,1)S(1)}, u32[]{:S(2)}, u32[]{:S(2)}) collective-permute-start(bf16[4,64,2304]{2,1,0:T(8,128)(2,1)S(1)} %get-tuple-element.22), channel_id=1, source_target_pairs={{0,8},{8,0},{16,24},{24,16},{1,9},{9,1},{17,25},{25,17},{2,10},{10... | collective-permute-start | bytes 3538952 | tf_op jit(solution)/shard_map/ppermute | solution.py:25
  27.0 38.9 %collective-permute-start.8 = (bf16[4,64,2304]{2,1,0:T(8,128)(2,1)S(1)}, bf16[4,64,2304]{2,1,0:T(8,128)(2,1)S(1)}, u32[]{:S(2)}, u32[]{:S(2)}) collective-permute-start(bf16[4,64,2304]{2,1,0:T(8,128)(2,1)S(1)} %get-tuple-element.23), channel_id=1, source_target_pairs={{0,16},{8,24},{16,0},{24,8},{1,17},{9,25},{17,1},{25,9},{2,18},{10... | collective-permute-start | bytes 3538952 | tf_op jit(solution)/shard_map/ppermute | solution.py:25
  39.2 27.2 %collective-permute-start.11 = (bf16[2,256,1024]{2,1,0:T(8,128)(2,1)}, bf16[2,256,1024]{2,1,0:T(8,128)(2,1)S(1)}, u32[]{:S(2)}, u32[]{:S(2)}) collective-permute-start(bf16[2,256,1024]{2,1,0:T(8,128)(2,1)} %collective-permute-done.10.refs_3_), channel_id=1, source_target_pairs={{0,8},{8,0},{16,24},{24,16},{1,9},{9,1},{17,25},{25,17},{2,10},{10... | collective-permute-start | bytes 3145736 | tf_op jit(solution)/shard_map/ppermute | solution.py:25
  41.1 25.4 %collective-permute-start.12 = (bf16[2,256,1024]{2,1,0:T(8,128)(2,1)S(1)}, bf16[2,256,1024]{2,1,0:T(8,128)(2,1)}, u32[]{:S(2)}, u32[]{:S(2)}) collective-permute-start(bf16[2,256,1024]{2,1,0:T(8,128)(2,1)S(1)} %collective-permute-done.2.refs_7_.refs_9_.refs_3_), channel_id=1, source_target_pairs={{0,2},{2,4},{4,6},{8,10},{10,12},{12,14},{16,18},{18,20},{20,22},{... | collective-permute-start | bytes 3145736 | tf_op jit(solution)/shard_map/ppermute | solution.py:25
  42.7 25.9 %collective-permute-start.3 = (bf16[2,256,1024]{2,1,0:T(8,128)(2,1)S(1)}, bf16[2,256,1024]{2,1,0:T(8,128)(2,1)S(1)}, u32[]{:S(2)}, u32[]{:S(2)}) collective-permute-start(bf16[2,256,1024]{2,1,0:T(8,128)(2,1)S(1)} %collective-permute-done.2.refs_7_.refs_9_.refs_3_), channel_id=1, source_target_pairs={{2,0},{3,1},{4,2},{5,3},{6,4},{7,5},{10,8},{11,9},{12,10},{13,11},... | collective-permute-start | bytes 3145736 | tf_op jit(solution)/shard_map/ppermute | solution.py:25
  44.0 49.4 %collective-permute-start.5 = (bf16[2,256,1024]{2,1,0:T(8,128)(2,1)}, bf16[2,256,1024]{2,1,0:T(8,128)(2,1)}, u32[]{:S(2)}, u32[]{:S(2)}) collective-permute-start(bf16[2,256,1024]{2,1,0:T(8,128)(2,1)} %collective-permute-done.refs_13_.refs_3_), channel_id=1, source_target_pairs={{2,1},{4,3},{6,5},{10,9},{12,11},{14,13},{18,17},{20,19},{22,21},{... | collective-permute-start | bytes 3145736 | tf_op jit(solution)/shard_map/ppermute | solution.py:25
  65.9 31.3 %collective-permute-start.14 = (bf16[2,256,1024]{2,1,0:T(8,128)(2,1)S(1)}, bf16[2,256,1024]{2,1,0:T(8,128)(2,1)S(1)}, u32[]{:S(2)}, u32[]{:S(2)}) collective-permute-start(bf16[2,256,1024]{2,1,0:T(8,128)(2,1)S(1)} %collective-permute-done.2.refs_7_.refs_9_.refs_3_), channel_id=1, source_target_pairs={{0,8},{8,0},{16,24},{24,16},{1,9},{9,1},{17,25},{25,17},{2,10},{10... | collective-permute-start | bytes 3145736 | tf_op jit(solution)/shard_map/ppermute | solution.py:25
  66.4 30.8 %collective-permute-start.1 = (bf16[2,256,1024]{2,1,0:T(8,128)(2,1)}, bf16[2,256,1024]{2,1,0:T(8,128)(2,1)}, u32[]{:S(2)}, u32[]{:S(2)}) collective-permute-start(bf16[2,256,1024]{2,1,0:T(8,128)(2,1)} %collective-permute-done.refs_13_.refs_3_), channel_id=1, source_target_pairs={{0,8},{8,0},{16,24},{24,16},{1,9},{9,1},{17,25},{25,17},{2,10},{10... | collective-permute-start | bytes 3145736 | tf_op jit(solution)/shard_map/ppermute | solution.py:25
  66.4 30.7 %collective-permute-start.13 = (bf16[2,256,1024]{2,1,0:T(8,128)(2,1)}, bf16[2,256,1024]{2,1,0:T(8,128)(2,1)}, u32[]{:S(2)}, u32[]{:S(2)}) collective-permute-start(bf16[2,256,1024]{2,1,0:T(8,128)(2,1)} %collective-permute-done.12.refs_5_), channel_id=1, source_target_pairs={{0,8},{8,0},{16,24},{24,16},{1,9},{9,1},{17,25},{25,17},{2,10},{10... | collective-permute-start | bytes 3145736 | tf_op jit(solution)/shard_map/ppermute | solution.py:25
  68.6 28.5 %collective-permute-start.4 = (bf16[2,256,1024]{2,1,0:T(8,128)(2,1)S(1)}, bf16[2,256,1024]{2,1,0:T(8,128)(2,1)}, u32[]{:S(2)}, u32[]{:S(2)}) collective-permute-start(bf16[2,256,1024]{2,1,0:T(8,128)(2,1)S(1)} %collective-permute-done.3.refs_11_.refs_3_.refs_5_), channel_id=1, source_target_pairs={{0,8},{8,0},{16,24},{24,16},{1,9},{9,1},{17,25},{25,17},{2,10},{10... | collective-permute-start | bytes 3145736 | tf_op jit(solution)/shard_map/ppermute | solution.py:25
  93.4 19.7 %collective-permute-start.6 = (bf16[2,256,1024]{2,1,0:T(8,128)(2,1)}, bf16[2,256,1024]{2,1,0:T(8,128)(2,1)}, u32[]{:S(2)}, u32[]{:S(2)}) collective-permute-start(bf16[2,256,1024]{2,1,0:T(8,128)(2,1)} %collective-permute-done.5.refs_5_.refs_7_), channel_id=1, source_target_pairs={{0,8},{8,0},{16,24},{24,16},{1,9},{9,1},{17,25},{25,17},{2,10},{10... | collective-permute-start | bytes 3145736 | tf_op jit(solution)/shard_map/ppermute | solution.py:25
  138.8 21.2 %collective-permute-start.19 = (bf16[4,64,768]{2,1,0:T(8,128)(2,1)}, bf16[4,64,768]{2,1,0:T(8,128)(2,1)S(1)}, u32[]{:S(2)}, u32[]{:S(2)}) collective-permute-start(bf16[4,64,768]{2,1,0:T(8,128)(2,1)} %get-tuple-element.17.refs_1_), channel_id=1, source_target_pairs={{0,16},{8,24},{16,0},{24,8},{1,17},{9,25},{17,1},{25,9},{2,18},{10... | collective-permute-start | bytes 1179656 | tf_op jit(solution)/shard_map/ppermute | solution.py:25
  140.1 17.6 %collective-permute-start.22 = (bf16[4,64,768]{2,1,0:T(8,128)(2,1)S(1)}, bf16[4,64,768]{2,1,0:T(8,128)(2,1)S(1)}, u32[]{:S(2)}, u32[]{:S(2)}) collective-permute-start(bf16[4,64,768]{2,1,0:T(8,128)(2,1)S(1)} %copy-done.14), channel_id=1, source_target_pairs={{0,16},{8,24},{16,0},{24,8},{1,17},{9,25},{17,1},{25,9},{2,18},{10... | collective-permute-start | bytes 1179656 | tf_op jit(solution)/shard_map/ppermute | solution.py:25
  148.8 17.3 %collective-permute-start.16 = (bf16[4,64,768]{2,1,0:T(8,128)(2,1)}, bf16[4,64,768]{2,1,0:T(8,128)(2,1)S(1)}, u32[]{:S(2)}, u32[]{:S(2)}) collective-permute-start(bf16[4,64,768]{2,1,0:T(8,128)(2,1)} %get-tuple-element.16.refs_1_), channel_id=1, source_target_pairs={{0,16},{8,24},{16,0},{24,8},{1,17},{9,25},{17,1},{25,9},{2,18},{10... | collective-permute-start | bytes 1179656 | tf_op jit(solution)/shard_map/ppermute | solution.py:25
  150.4 17.1 %collective-permute-start.21 = (bf16[4,64,768]{2,1,0:T(8,128)(2,1)S(1)}, bf16[4,64,768]{2,1,0:T(8,128)(2,1)}, u32[]{:S(2)}, u32[]{:S(2)}) collective-permute-start(bf16[4,64,768]{2,1,0:T(8,128)(2,1)S(1)} %copy-done.14), channel_id=1, source_target_pairs={{0,8},{8,0},{16,24},{24,16},{1,9},{9,1},{17,25},{25,17},{2,10},{10... | collective-permute-start | bytes 1179656 | tf_op jit(solution)/shard_map/ppermute | solution.py:25
  151.2 22.4 %collective-permute-start.18 = (bf16[4,64,768]{2,1,0:T(8,128)(2,1)S(1)}, bf16[4,64,768]{2,1,0:T(8,128)(2,1)S(1)}, u32[]{:S(2)}, u32[]{:S(2)}) collective-permute-start(bf16[4,64,768]{2,1,0:T(8,128)(2,1)S(1)} %copy-done.7), channel_id=1, source_target_pairs={{0,8},{8,0},{16,24},{24,16},{1,9},{9,1},{17,25},{25,17},{2,10},{10... | collective-permute-start | bytes 1179656 | tf_op jit(solution)/shard_map/ppermute | solution.py:25
  157.7 13.0 %collective-permute-start.23 = (bf16[4,64,768]{2,1,0:T(8,128)(2,1)S(1)}, bf16[4,64,768]{2,1,0:T(8,128)(2,1)}, u32[]{:S(2)}, u32[]{:S(2)}) collective-permute-start(bf16[4,64,768]{2,1,0:T(8,128)(2,1)S(1)} %collective-permute-done.22.refs_3_), channel_id=1, source_target_pairs={{0,8},{8,0},{16,24},{24,16},{1,9},{9,1},{17,25},{25,17},{2,10},{10... | collective-permute-start | bytes 1179656 | tf_op jit(solution)/shard_map/ppermute | solution.py:25
  160.1 13.6 %collective-permute-start.20 = (bf16[4,64,768]{2,1,0:T(8,128)(2,1)S(1)}, bf16[4,64,768]{2,1,0:T(8,128)(2,1)S(1)}, u32[]{:S(2)}, u32[]{:S(2)}) collective-permute-start(bf16[4,64,768]{2,1,0:T(8,128)(2,1)S(1)} %collective-permute-done.19.refs_3_), channel_id=1, source_target_pairs={{0,8},{8,0},{16,24},{24,16},{1,9},{9,1},{17,25},{25,17},{2,10},{10... | collective-permute-start | bytes 1179656 | tf_op jit(solution)/shard_map/ppermute | solution.py:25
  166.1 11.9 %collective-permute-start.15 = (bf16[4,64,768]{2,1,0:T(8,128)(2,1)}, bf16[4,64,768]{2,1,0:T(8,128)(2,1)S(1)}, u32[]{:S(2)}, u32[]{:S(2)}) collective-permute-start(bf16[4,64,768]{2,1,0:T(8,128)(2,1)} %get-tuple-element.16.refs_1_), channel_id=1, source_target_pairs={{0,8},{8,0},{16,24},{24,16},{1,9},{9,1},{17,25},{25,17},{2,10},{10... | collective-permute-start | bytes 1179656 | tf_op jit(solution)/shard_map/ppermute | solution.py:25
  167.5 10.5 %collective-permute-start.17 = (bf16[4,64,768]{2,1,0:T(8,128)(2,1)S(1)}, bf16[4,64,768]{2,1,0:T(8,128)(2,1)S(1)}, u32[]{:S(2)}, u32[]{:S(2)}) collective-permute-start(bf16[4,64,768]{2,1,0:T(8,128)(2,1)S(1)} %collective-permute-done.16.refs_3_), channel_id=1, source_target_pairs={{0,8},{8,0},{16,24},{24,16},{1,9},{9,1},{17,25},{25,17},{2,10},{10... | collective-permute-start | bytes 1179656 | tf_op jit(solution)/shard_map/ppermute | solution.py:25
  (17 other events, 338.9 us)
